TPU v7x, 128 devices: a whole 4x4x4 slice. The times are simulated.
128 devices in a mesh: dp: 8 (over z_lo, x), expert: 16 (over y, z_hi, core).
Axes of the slice: x: 4, y: 4, z: 4 (z_hi: 2, z_lo: 2; z = z_hi * 2 + z_lo), core: 2. Of those that a mesh axis runs over, the one named last changes fastest.
Arguments:
- hidden: bfloat16 [16, 9216, 1408], P('expert', 'dp')
- upstream: bfloat16 [16, 9216, 2048], P('expert', 'dp')
- token_counts: int32 [16, 8], P('expert', 'dp'), may hold values from 1 to 1152, as said below
- master: float32 [16, 1408, 2048], P('expert', 'dp'), may hold values from -0.15625 to 0.15625
- first_moment: float32 [16, 1408, 2048], P('expert', 'dp'), may hold values from -6 to 6
- second_moment: float32 [16, 1408, 2048], P('expert', 'dp'), may hold values from 0.25 to 4
- router_input: bfloat16 [16384, 2048], P(('dp', 'expert')), may hold values from -6 to 6
- router_cot: bfloat16 [64, 16384], P(None, ('dp', 'expert'))
- router_master: float32 [64, 2048], replicated, may hold values from -0.125 to 0.125
- router_first: float32 [64, 2048], replicated, may hold values from -6 to 6
- router_second: float32 [64, 2048], replicated, may hold values from 0.25 to 4
- partner: int32 [16], replicated, may hold values from 0 to 15, as said below
Outputs:
- new_weight: bfloat16 [16, 1408, 2048], P('expert')
- new_master: float32 [16, 1408, 2048], P('expert', 'dp')
- new_first: float32 [16, 1408, 2048], P('expert', 'dp')
- new_second: float32 [16, 1408, 2048], P('expert', 'dp')
- router_master_new: float32 [64, 2048], replicated
- router_first_new: float32 [64, 2048], replicated
- router_second_new: float32 [64, 2048], replicated
Inputs may be any that keep to these rules, and one draw needn't show every extreme that they name: partner[partner[p]] = p for every position p; a position with partner[p] = p keeps its expert. The first token_counts[e, d] of replica d's 1152 slots for position e are live, the rest are padding.
All inputs are finite; a program needn't handle non-finite values.
Results may differ from a plain program's by a relative error of at most 0.001.
Values may be sent and summed in bfloat16 or wider, within the bound.
A program may use at most 128 MiB of HBM per device.

v0:
```python
import math

import jax
import jax.numpy as jnp
from jax import lax
from jax.sharding import Mesh
from jax.sharding import PartitionSpec as P

DP = ("dp_0", "dp_1")
DP_EXPERT = ("dp_0", "dp_1", "expert")


beta_first = 0.9
beta_second = 0.95
learn_rate = 0.001
decay_weight = 0.1
adam_eps = 1e-08
norm_eps = 1e-06
correct_first = 1.0 - 0.9**10
correct_second = 1.0 - 0.95**10


def laid_out(tiles, dim):
    tiles = jnp.moveaxis(tiles, 0, dim)
    shape = tiles.shape
    return tiles.reshape(*shape[:dim], shape[dim] * shape[dim + 1], *shape[dim + 2 :])


def gather_in_order(shard, axes, turns):
    tiles = shard
    for k in turns:
        tiles = lax.all_gather(tiles, axes[k])
    done = turns[::-1]
    back = [done.index(k) for k in range(len(axes))]
    tiles = tiles.transpose(*back, *range(len(axes), tiles.ndim))
    return tiles.reshape(-1, *shard.shape)


def gather_axes(shard, axes, turns, dim):
    return laid_out(gather_in_order(shard, axes, turns), dim)


def together(arrays, axis):
    vector, at, done = (jnp.concatenate([a.reshape(-1) for a in arrays]), 0, [])
    total = lax.psum(vector, axis)
    for a in arrays:
        done.append(total[at : at + a.size].reshape(a.shape))
        at += a.size
    return tuple(done)


def adam_update(gradient, moment_one, moment_two, weights):
    first_new = beta_first * moment_one + (1.0 - beta_first) * gradient
    second_new = beta_second * moment_two + (1.0 - beta_second) * gradient * gradient
    ratio = first_new / correct_first / (jnp.sqrt(second_new / correct_second) + adam_eps)
    weights_new = weights - learn_rate * (ratio + decay_weight * weights)
    return (weights_new, first_new, second_new)


def split_pieces(matrix, groups):
    return matrix.reshape(matrix.shape[0], groups, matrix.shape[1] // groups)


def relocate_state(states, partner):
    groups = lax.axis_size("expert")
    pieces = tuple((split_pieces(member, groups) for member in states))

    def reorder(received):
        arranged = tuple((jnp.take(member, partner, axis=1) for member in received))
        return lax.all_to_all(arranged, "expert", split_axis=1, concat_axis=1, tiled=True)

    result = reorder(
        (
            lax.all_to_all(pieces[0], "expert", split_axis=1, concat_axis=1, tiled=True),
            lax.all_to_all(pieces[1], "expert", split_axis=1, concat_axis=1, tiled=True),
            lax.all_to_all(pieces[2], "expert", split_axis=1, concat_axis=1, tiled=True),
        )
    )
    return tuple((member.reshape(member.shape[0], -1) for member in result))


def regather(weight_shard):
    return gather_axes(weight_shard, DP, (0, 1), 0)


def on_device(
    hidden,
    upstream,
    token_counts,
    master,
    first_moment,
    second_moment,
    router_input,
    router_cot,
    router_master,
    router_first,
    router_second,
    partner,
):
    hidden_units = hidden.shape[2]
    features = upstream.shape[2]
    row_count = hidden.shape[1]
    live_rows = jnp.arange(row_count, dtype=jnp.int32) < token_counts[0, 0]
    activations = hidden[0]
    grads_out = upstream[0]
    masked_out = jnp.where(live_rows[:, None], grads_out, jnp.zeros_like(grads_out))
    router_partial = jnp.dot(router_cot, router_input, preferred_element_type=jnp.float32)
    gradient = lax.psum_scatter(
        lax.dot_general(
            activations, masked_out, (((0,), (0,)), ((), ())), preferred_element_type=jnp.float32
        ),
        DP,
        scatter_dimension=0,
        tiled=True,
    )
    router_grad, expert_square = together((router_partial, jnp.sum(gradient * gradient)), DP_EXPERT)
    total_square = expert_square + jnp.sum(router_grad * router_grad)
    clip_limit = 2.0 * math.sqrt(
        float(lax.axis_size("expert") * hidden_units * features + router_cot.shape[0] * features)
    )
    factor = jnp.minimum(1.0, clip_limit / (jnp.sqrt(total_square) + norm_eps))
    master_new, first_new, second_new = adam_update(
        factor * gradient, first_moment[0], second_moment[0], master[0]
    )
    router_outs = adam_update(factor * router_grad, router_first, router_second, router_master)
    moved = relocate_state((master_new, first_new, second_new), partner)
    moved_weight = regather(moved[0].astype(jnp.bfloat16))
    return (
        moved_weight[None],
        moved[0][None],
        moved[1][None],
        moved[2][None],
        router_outs[0],
        router_outs[1],
        router_outs[2],
    )


def solution(mesh):
    split = Mesh(mesh.devices.reshape(2, 4, mesh.shape["expert"]), ("dp_0", "dp_1", "expert"))
    return jax.shard_map(
        on_device,
        mesh=split,
        in_specs=(
            P("expert", DP, None),
            P("expert", DP, None),
            P("expert", DP),
            P("expert", DP, None),
            P("expert", DP, None),
            P("expert", DP, None),
            P(DP_EXPERT, None),
            P(None, DP_EXPERT),
            P(),
            P(),
            P(),
            P(),
        ),
        out_specs=(
            P("expert", None, None),
            P("expert", DP, None),
            P("expert", DP, None),
            P("expert", DP, None),
            P(),
            P(),
            P(),
        ),
        check_vma=False,
    )
```

profile of v0, /device:TPU:1, one launch (start us, length us, event | category | flops | bytes accessed | tf_op | source)
XLA Modules:
  0.0 538.0 jit_solution(12139211565986027123)
XLA Ops:
  7.2 0.0 copy-start
  7.2 0.0 reduce-scatter.4.cloned.1.call-start
  8.0 1.1 copy-done
  9.1 12.9 %convolution_bitcast_fusion = f32[1408,2048]{0,1:T(8,128)} fusion(bf16[1,1152,2048]{2,1,0:T(8,128)(2,1)} %param.15, pred[1152]{0:T(1024)(128)(4,1)S(1)} %iota_compare_fusion, bf16[1,1152,1408]{2,1,0:T(8,128)(2,1)S(1)} %copy-done), kind=kOutput, calls=%fused_computation.3 | convolution fusion | flops 6646136832 | bytes 19498112 | tf_op jit(solution)/shard_map/dot_general | solution.py:109
  22.0 12.0 %copy.43 = f32[1408,2048]{1,0:T(8,128)} copy(f32[1408,2048]{0,1:T(8,128)} %convolution_bitcast_fusion) | data formatting | bytes 23068672
  34.0 0.0 copy-start.6
  34.0 0.0 reduce-scatter.4.cloned.1.call-update
  34.0 0.0 all-reduce.2.cloned.1.call-start
  34.1 1.0 copy-done.5
  35.0 0.0 copy-done.6
  35.0 0.2 convolution_bitcast_fusion.1
  35.3 0.1 copy.45
  35.4 124.4 %reduce-scatter.4.cloned.1.call-done = f32[176,2048]{1,0:T(8,128)} async-done(((f32[1408,2048]{1,0:T(8,128)}), f32[176,2048]{1,0:T(8,128)}) %reduce-scatter.4.cloned.1.call-update) | async-done | bytes 1441808
  159.8 1.8 copy.44
  161.6 1.1 multiply_reduce_fusion
  162.7 1.5 pad_maximum_fusion
  164.2 0.0 all-reduce.2.cloned.1.call-update
  164.2 2.8 copy.33
  167.0 2.8 copy.34
  169.8 2.8 copy.35
  172.6 137.9 %all-reduce.2.cloned.1.call-done = f32[131073]{0:T(1024)} async-done(((f32[131073]{0:T(1024)}), f32[131073]{0:T(1024)}) %all-reduce.2.cloned.1.call-update) | async-done | bytes 524308 | tf_op jit(solution)/shard_map/psum | solution.py:45
  310.5 1.2 slice.14
  311.7 1.8 multiply_reduce_fusion.1
  314.9 6.6 %bitcast_subtract_fusion = (f32[176,2048]{0,1:T(8,128)}, f32[176,2048]{0,1:T(8,128)}, f32[176,2048]{0,1:T(8,128)}) fusion(f32[1,176,2048]{1,2,0:T(8,128)} %copy.33, f32[176,2048]{0,1:T(8,128)S(1)} %copy.44, f32[]{:T(128)S(6)} %min_shard_map.3, f32[1,176,2048]{1,2,0:T(8,128)} %copy.34, f32[1,176,2048]{1,2,0:T(8,128)} %copy.35), kind=kLoop, calls=%fused_computation.12 | loop fusion | flops 5767168 | bytes 10092548 | tf_op jit(solution)/shard_map/sub | solution.py:56
  321.5 2.8 copy.36
  324.2 5.4 %all-to-all-start = ((f32[176,16,128]{2,0,1:T(8,128)}), f32[176,16,128]{2,0,1:T(8,128)}, u32[]{:S(2)}, u32[]{:S(2)}) async-start(f32[176,16,128]{2,0,1:T(8,128)} %copy.36), calls=%async_computation | async-start | bytes 2883584 | tf_op jit(solution)/shard_map/all_to_all | solution.py:74
  329.6 0.0 copy-done.3
  329.6 1.7 copy.39
  331.3 19.7 %all-to-all-done = f32[176,16,128]{2,0,1:T(8,128)} async-done(((f32[176,16,128]{2,0,1:T(8,128)}), f32[176,16,128]{2,0,1:T(8,128)}, u32[]{:S(2)}, u32[]{:S(2)}) %all-to-all-start) | async-done | bytes 1441824 | tf_op jit(solution)/shard_map/all_to_all | solution.py:74
  351.0 5.1 all-to-all-start.2
  356.1 0.0 copy-done.2
  356.1 1.7 copy.41
  357.8 19.8 %all-to-all-done.2 = f32[176,16,128]{2,0,1:T(8,128)} async-done(((f32[176,16,128]{2,0,1:T(8,128)}), f32[176,16,128]{2,0,1:T(8,128)}, u32[]{:S(2)}, u32[]{:S(2)}) %all-to-all-start.2) | async-done | bytes 1441824 | tf_op jit(solution)/shard_map/all_to_all | solution.py:75
  377.6 4.6 all-to-all-start.4
  382.2 0.0 all-gather.4.cloned.1.call-start
  382.2 0.0 copy-done.7
  382.3 2.0 gather_fusion
  384.3 3.1 gather_fusion.1
  387.4 16.1 %all-to-all-done.4 = f32[176,16,128]{2,0,1:T(8,128)S(1)} async-done(((f32[176,16,128]{2,0,1:T(8,128)}), f32[176,16,128]{2,0,1:T(8,128)S(1)}, u32[]{:S(2)}, u32[]{:S(2)}) %all-to-all-start.4) | async-done | bytes 1441824 | tf_op jit(solution)/shard_map/all_to_all | solution.py:76
  403.5 1.7 gather_fusion.2
  405.2 3.8 select_bitcast_fusion
  409.0 25.8 %all_to_all.30 = f32[176,16,128]{2,0,1:T(8,128)S(1)} all-to-all(f32[176,16,128]{2,0,1:T(8,128)S(1)} %get-tuple-element.16), channel_id=1, replica_groups=mesh['dp_0'=2,'dp_1'=4,'expert'=16] {'expert'}, dimensions={1} | all-to-all | bytes 2883584 | tf_op jit(solution)/shard_map/all_to_all | solution.py:70
  434.8 0.5 copy.37
  435.2 0.2 reshape.73
  435.4 0.0 copy-start.4
  435.5 1.1 convert_element_type.10
  436.5 0.0 all-gather.4.cloned.1.call-update
  436.6 0.0 all-gather.6.cloned.1.call-start
  436.6 24.8 %all-gather.4.cloned.1.call-done = bf16[2,176,2048]{2,1,0:T(8,128)(2,1)} async-done(((bf16[1,176,2048]{2,1,0:T(8,128)(2,1)}), bf16[2,176,2048]{2,1,0:T(8,128)(2,1)}) %all-gather.4.cloned.1.call-update) | async-done | bytes 1441808 | tf_op jit(solution)/shard_map/all_gather | solution.py:32
  461.4 0.0 all-gather.6.cloned.1.call-update
  461.4 0.0 copy-done.4
  461.5 28.8 %all_to_all.31 = f32[176,16,128]{2,0,1:T(8,128)S(1)} all-to-all(f32[176,16,128]{2,0,1:T(8,128)} %get-tuple-element.15), channel_id=1, replica_groups=mesh['dp_0'=2,'dp_1'=4,'expert'=16] {'expert'}, dimensions={1} | all-to-all | bytes 2883584 | tf_op jit(solution)/shard_map/all_to_all | solution.py:70
  490.2 4.1 all-to-all-start.5
  494.3 1.9 slice_multiply_fusion
  496.2 1.9 mul.115
  498.1 2.9 multiply_subtract_fusion
  501.0 1.5 copy.40
  502.6 2.5 broadcast_in_dim_reshape.7
  505.1 10.6 %all-to-all-done.5 = f32[176,16,128]{2,0,1:T(8,128)S(1)} async-done(((f32[176,16,128]{2,0,1:T(8,128)}), f32[176,16,128]{2,0,1:T(8,128)S(1)}, u32[]{:S(2)}, u32[]{:S(2)}) %all-to-all-start.5) | async-done | bytes 1441824 | tf_op jit(solution)/shard_map/all_to_all | solution.py:70
  515.7 0.5 copy.42
  516.2 1.3 broadcast_in_dim_reshape.8
  517.5 7.7 %all-gather.6.cloned.1.call-done = bf16[8,176,2048]{2,1,0:T(8,128)(2,1)} async-done(((bf16[2,176,2048]{2,1,0:T(8,128)(2,1)}), bf16[8,176,2048]{2,1,0:T(8,128)(2,1)}) %all-gather.6.cloned.1.call-update) | async-done | bytes 5767184 | tf_op jit(solution)/shard_map/all_gather | solution.py:32
  525.2 6.3 %copy.38 = bf16[2,4,176,2048]{3,2,1,0:T(8,128)(2,1)} copy(bf16[2,4,176,2048]{3,2,0,1:T(8,128)(2,1)} %bitcast.49) | data formatting | bytes 11534336 | tf_op jit(solution)/shard_map/transpose | solution.py:35
  531.5 0.0 copy-done.1
  (9 shorter events, 0.0 us)
Async XLA Ops:
  7.2 1.9 copy-start
  7.2 152.6 %reduce-scatter.4.cloned.1.call-start = ((), (), s32[]{:S(2)}) async-start(), calls=%async_computation.10 | async-start | bytes 12976128
  34.0 1.0 copy-start.5
  34.0 1.0 copy-start.6
  34.0 276.5 %all-reduce.2.cloned.1.call-start = ((), (), s32[]{:S(2)}) async-start(), calls=%async_computation.7 | async-start | bytes 1056768 | tf_op jit(solution)/shard_map/psum | solution.py:45
  324.2 5.4 %copy-start.3 = (f32[176,2048]{0,1:T(8,128)S(1)}, f32[176,2048]{0,1:T(8,128)}, u32[]{:S(2)}) copy-start(f32[176,2048]{0,1:T(8,128)} %get-tuple-element.12) | copy-start | bytes 4325380
  324.2 26.8 %all-to-all-start = ((f32[176,16,128]{2,0,1:T(8,128)}), f32[176,16,128]{2,0,1:T(8,128)}, u32[]{:S(2)}, u32[]{:S(2)}) async-start(f32[176,16,128]{2,0,1:T(8,128)} %copy.36), calls=%async_computation | async-start | bytes 2883584 | tf_op jit(solution)/shard_map/all_to_all | solution.py:74
  331.3 24.8 %copy-start.2 = (f32[176,2048]{0,1:T(8,128)S(1)}, f32[176,2048]{0,1:T(8,128)}, u32[]{:S(2)}) copy-start(f32[176,2048]{0,1:T(8,128)} %get-tuple-element.13) | copy-start | bytes 4325380
  351.0 26.6 %all-to-all-start.2 = ((f32[176,16,128]{2,0,1:T(8,128)}), f32[176,16,128]{2,0,1:T(8,128)}, u32[]{:S(2)}, u32[]{:S(2)}) async-start(f32[176,16,128]{2,0,1:T(8,128)} %copy.39), calls=%async_computation.2 | async-start | bytes 2883584 | tf_op jit(solution)/shard_map/all_to_all | solution.py:75
  357.8 24.4 %copy-start.7 = (s32[16]{0:T(128)S(1)}, s32[16]{0:T(128)}, u32[]{:S(2)}) copy-start(s32[16]{0:T(128)} %param.25) | copy-start | bytes 196
  377.6 25.8 %all-to-all-start.4 = ((f32[176,16,128]{2,0,1:T(8,128)}), f32[176,16,128]{2,0,1:T(8,128)S(1)}, u32[]{:S(2)}, u32[]{:S(2)}) async-start(f32[176,16,128]{2,0,1:T(8,128)} %copy.41), calls=%async_computation.4 | async-start | bytes 2883584 | tf_op jit(solution)/shard_map/all_to_all | solution.py:76
  382.2 79.3 %all-gather.4.cloned.1.call-start = ((), (), s32[]{:S(2)}) async-start(), calls=%async_computation.8 | async-start | bytes 2162688 | tf_op jit(solution)/shard_map/all_gather | solution.py:32
  435.4 26.0 %copy-start.4 = (f32[1,176,2048]{2,1,0:T(8,128)}, f32[1,176,2048]{2,1,0:T(8,128)S(1)}, u32[]{:S(2)}) copy-start(f32[1,176,2048]{2,1,0:T(8,128)S(1)} %reshape.73) | copy-start | bytes 4325380
  436.6 88.6 %all-gather.6.cloned.1.call-start = ((), (), s32[]{:S(2)}) async-start(), calls=%async_computation.9 | async-start | bytes 7208960 | tf_op jit(solution)/shard_map/all_gather | solution.py:32
  490.2 25.5 %all-to-all-start.5 = ((f32[176,16,128]{2,0,1:T(8,128)}), f32[176,16,128]{2,0,1:T(8,128)S(1)}, u32[]{:S(2)}, u32[]{:S(2)}) async-start(f32[176,16,128]{2,0,1:T(8,128)} %get-tuple-element.14), calls=%async_computation.5 | async-start | bytes 2883584 | tf_op jit(solution)/shard_map/all_to_all | solution.py:70
  525.2 6.3 %copy-start.1 = (bf16[1,1152,1408]{2,1,0:T(8,128)(2,1)S(1)}, bf16[1,1152,1408]{2,1,0:T(8,128)(2,1)}, u32[]{:S(2)}) copy-start(bf16[1,1152,1408]{2,1,0:T(8,128)(2,1)} %param.14) | copy-start | bytes 9732100
Sparse Core Ops, SparseCore 0:
  34.1 125.5 reduce-scatter.3
  165.1 145.3 all-reduce.1
  436.7 24.6 all-gather.3
  462.9 62.2 all-gather.5
where the time goes:
time: 539 us; the launch traced here: 538 us
  waiting for transfers between devices  361 us (67%)
  blocking collectives  54.5 us (10%)
  local copies, waits for them, and re-layouts  53.2 us (10%)
  other arithmetic  20.7 us (4%)
  starting transfers between devices  19.3 us (4%)
  between operations  16.1 us (3%)
  matrix products  13.1 us (2%)
    psum x1, waiting for transfers between devices, together(): total = lax.psum(vector, axis)  138 us
    unnamed x5, waiting for transfers between devices  124 us
    all_to_all x2, blocking collectives, reorder(): lax.all_to_all(arranged, 'expert', split_axis=1, concat_axis=1, tiled=True)  54.5 us
    all_gather x2, waiting for transfers between devices, gather_in_order(): tiles = lax.all_gather(tiles, axes[k])  32.5 us
    unnamed x22, local copies, waits for them, and re-layouts  24.3 us
    all_to_all x1, waiting for transfers between devices, relocate_state(): lax.all_to_all(pieces[1], 'expert', split_axis=1, concat_axis=1, tiled=True)  19.8 us
    all_to_all x1, waiting for transfers between devices, relocate_state(): lax.all_to_all(pieces[0], 'expert', split_axis=1, concat_axis=1, tiled=True)  19.7 us
    all_to_all x1, waiting for transfers between devices, relocate_state(): lax.all_to_all(pieces[2], 'expert', split_axis=1, concat_axis=1, tiled=True)  16.1 us
  transfers between devices with their start and end apart: 8, of which 8 were waited for; matrix products, arithmetic and copies ran while one was open for 6% of the time, Pallas kernels for 0%

commit v1 on v0

v1 whole, which is shorter than its diff:
```python
import functools
import math

import jax
import jax.numpy as jnp
from jax import lax
from jax.experimental import pallas as pl
from jax.experimental.pallas import tpu as pltpu
from jax.sharding import Mesh
from jax.sharding import PartitionSpec as P

MESH = pl.DeviceIdType.MESH
DP = ("zl", "x")
ALL = ("zl", "x", "e")
F32 = jnp.float32
I16 = jnp.int16

beta_first = 0.9
beta_second = 0.95
learn_rate = 0.001
decay_weight = 0.1
adam_eps = 1e-08
norm_eps = 1e-06
correct_first = 1.0 - 0.9**10
correct_second = 1.0 - 0.95**10

GROUPS = 16
LANES = 128
TOP = 15.0
SMALL = 2.0**-100


def code_of(peak):
    return jnp.ceil(16.0 * jnp.log2(jnp.maximum(peak, SMALL)))


def to_codes(values, code):
    scaled = jnp.round(values * jnp.exp2(TOP - code * (1.0 / 16.0)))
    return jnp.clip(scaled, -32767.0, 32767.0).astype(I16)


def scale_of(code):
    return jnp.exp2(code * (1.0 / 16.0) - TOP)


def encode_rows(values, dst, rows):
    width = values.shape[1]
    code = code_of(jnp.max(jnp.abs(values), axis=1, keepdims=True))
    dst[rows, :width] = to_codes(values, code)
    dst[rows, width:] = jnp.broadcast_to(code, (values.shape[0], LANES)).astype(I16)


def decode_rows(src, rows, width):
    code = src[rows, width : width + LANES].astype(F32)[:, :1]
    return src[rows, :width].astype(F32) * scale_of(code)


def cut(rows):
    tiles = rows // 16
    first = (tiles + 1) // 2 * 16
    return ((0, first), (first, rows - first))


def send(src, dst, send_sem, recv_sem, device):
    copy = pltpu.make_async_remote_copy(
        src_ref=src, dst_ref=dst, send_sem=send_sem, recv_sem=recv_sem, device_id=device, device_id_type=MESH
    )
    copy.start()
    return copy


def reduce_kernel(
    hid,
    up,
    counts,
    cot,
    rin,
    grad,
    rgrad,
    total,
    hid_t,
    part,
    held,
    out_buf,
    in_buf,
    rp,
    rx,
    r1,
    rz,
    r2,
    ry,
    r3,
    rc,
    sums,
    ssem,
    rsem,
    r_ssem,
    r_rsem,
    n_ssem,
    n_rsem,
):
    zl, x, e = (lax.axis_index(a) for a in ALL)
    y, zh, core = e // 4, (e // 2) % 2, e % 2
    z = zh * 2 + zl
    depth, units = hid.shape
    wide = up.shape[1]
    rows = units // 8

    def at_x(j):
        return {"x": (x + j) % 4}

    def at_z(j):
        there = (z + j) % 4
        return {"zl": there % 2, "e": y * 4 + (there // 2) * 2 + core}

    def at_y(j):
        return {"e": ((y + j) % 4) * 4 + zh * 2 + core}

    def at_core(j):
        return {"e": e + 1 - 2 * core}

    def at_pair():
        return {"zl": 1 - zl}

    axes = ((at_x, 4, x), (at_z, 4, z), (at_y, 4, y), (at_core, 2, core))

    barrier = pltpu.get_barrier_semaphore()
    for at, size, _ in axes:
        for j in range(1, size):
            pl.semaphore_signal(barrier, inc=1, device_id=at(j), device_id_type=MESH)

    rp[...] = jnp.dot(cot[...], rin[...], preferred_element_type=F32)
    pl.semaphore_wait(barrier, 10)

    r_rows, r_cols = rp.shape[0] // 4, wide // 4
    stage0 = [
        send(
            rp.at[pl.ds(((x + j) % 4) * r_rows, r_rows)],
            rx.at[j - 1],
            r_ssem.at[0, j],
            r_rsem.at[0, j],
            at_x(j),
        )
        for j in range(1, 4)
    ]

    live = counts[0, 0]

    @pl.loop(0, units // LANES)
    def _(t):
        cols = pl.ds(pl.multiple_of(t * LANES, LANES), LANES)
        keep = lax.broadcasted_iota(jnp.int32, (depth, LANES), 0) < live
        tile = jnp.where(keep, hid[:, cols].astype(F32), 0.0).astype(jnp.bfloat16)
        hid_t[cols, :] = tile.T

    def multiply(block, dst):
        at = pl.multiple_of(block * rows, 16)

        @pl.loop(0, wide // 512)
        def _(n):
            cols = pl.ds(pl.multiple_of(n * 512, 512), 512)
            dst[:, cols] = jnp.dot(hid_t[pl.ds(at, rows), :], up[:, cols], preferred_element_type=F32)

    def encode(src, slot, run, *incoming):
        start, size = run

        @pl.loop(0, size // 16)
        def _(i):
            r = pl.ds(pl.multiple_of(start + i * 16, 16), 16)
            values = src[r, :]
            for b in incoming:
                values = values + decode_rows(in_buf.at[b], r, wide)
            encode_rows(values, out_buf.at[slot], r)

    def ship(slot, run, c, device):
        r = pl.ds(run[0], run[1])
        return send(out_buf.at[slot, r], in_buf.at[slot, r], ssem.at[slot, c], rsem.at[slot, c], device)

    runs = cut(rows)
    far, right, left = (x + 2) % 4, (x + 1) % 4, (x + 3) % 4
    copies = {}
    for slot, block, step in ((0, far, 3), (1, 4 + far, 1), (2, right, 1), (3, 4 + left, 3)):
        multiply(block, part)
        for c, run in enumerate(runs):
            encode(part, slot, run)
            copies[slot, c] = ship(slot, run, c, at_x(step))
    multiply(left, held.at[0])
    multiply(4 + right, held.at[1])

    for copy in stage0:
        copy.wait_recv()
    r1[...] = rp[pl.ds(x * r_rows, r_rows), :] + rx[0] + rx[1] + rx[2]
    stage1 = [
        send(
            r1.at[:, pl.ds(pl.multiple_of(((z + j) % 4) * r_cols, LANES), r_cols)],
            rz.at[j - 1],
            r_ssem.at[1, j],
            r_rsem.at[1, j],
            at_z(j),
        )
        for j in range(1, 4)
    ]

    for c, run in enumerate(runs):
        for slot, step in ((4, 3), (5, 1)):
            copies[slot - 4, c].wait_recv()
            encode(held.at[slot - 4], slot, run, slot - 4)
            copies[slot, c] = ship(slot, run, c, at_x(step))

    multiply(x, held.at[2])
    multiply(4 + x, held.at[3])

    for copy in stage1:
        copy.wait_recv()
    r2[...] = r1[:, pl.ds(pl.multiple_of(z * r_cols, LANES), r_cols)] + rz[0] + rz[1] + rz[2]
    stage2 = [
        send(
            r2.at[:, pl.ds(pl.multiple_of(((y + j) % 4) * LANES, LANES), LANES)],
            ry.at[j - 1],
            r_ssem.at[2, j],
            r_rsem.at[2, j],
            at_y(j),
        )
        for j in range(1, 4)
    ]
    for copy in stage2:
        copy.wait_recv()
    r3[...] = r2[:, pl.ds(pl.multiple_of(y * LANES, LANES), LANES)] + ry[0] + ry[1] + ry[2]
    other = pl.multiple_of((1 - core) * 8, 8)
    stage3 = send(r3.at[pl.ds(other, 8)], rc, r_ssem.at[3, 1], r_rsem.at[3, 1], at_core(1))

    for c, run in enumerate(runs):
        copies[2, c].wait_recv()
        copies[4, c].wait_recv()
        copies[3, c].wait_recv()
        copies[5, c].wait_recv()

        @pl.loop(0, run[1] // 16)
        def _(i, run=run):
            r = pl.ds(pl.multiple_of(run[0] + i * 16, 16), 16)
            held[2, r, :] += decode_rows(in_buf.at[2], r, wide) + decode_rows(in_buf.at[4], r, wide)
            held[3, r, :] += decode_rows(in_buf.at[3], r, wide) + decode_rows(in_buf.at[5], r, wide)

        encode(held.at[3 - zl], 6, run)
        copies[6, c] = ship(6, run, c, at_pair())

    stage3.wait_recv()
    piece = r3[pl.ds(pl.multiple_of(core * 8, 8), 8), :] + rc[...]
    my_rows, my_cols = x * r_rows + core * 8, z * r_cols + y * LANES
    rgrad[pl.ds(pl.multiple_of(my_rows, 8), 8), pl.ds(pl.multiple_of(my_cols, LANES), LANES)] = piece

    def spread(row, height, col, width, stage, at, size):
        part_of = rgrad.at[
            pl.ds(pl.multiple_of(row, 8), height), pl.ds(pl.multiple_of(col, LANES), width)
        ]
        return [
            send(part_of, part_of, r_ssem.at[stage, j], r_rsem.at[stage, j], at(j)) for j in range(1, size)
        ]

    back = [spread(my_rows, 8, my_cols, LANES, 4, at_core, 2)]

    squares = piece * piece
    for c, run in enumerate(runs):
        copies[6, c].wait_recv()

        def add(i, acc, run=run):
            r = pl.ds(pl.multiple_of(run[0] + i * 16, 16), 16)
            values = held[2 + zl, r, :] + decode_rows(in_buf.at[6], r, wide)
            grad[r, :] = values
            values = values * values
            for a in range(2):
                for b in range(wide // LANES):
                    acc = acc + values[a * 8 : a * 8 + 8, b * LANES : (b + 1) * LANES]
            return acc

        squares = lax.fori_loop(0, run[1] // 16, add, squares)

    norm_copies = []
    spreads = (
        (x * r_rows, 2 * 8, my_cols, LANES, 5, at_y, 4),
        (x * r_rows, r_rows, z * r_cols, r_cols, 6, at_z, 4),
        (x * r_rows, r_rows, 0, wide, 7, at_x, 4),
    )
    for stage, (at, size, here) in enumerate(axes):
        sums[stage, here] = squares
        mine = sums.at[stage, here]
        group = [
            send(mine, mine, n_ssem.at[stage, j], n_rsem.at[stage, j], at(j)) for j in range(1, size)
        ]
        norm_copies += group
        if stage < 3:
            for copy in back[-1]:
                copy.wait_recv()
            back.append(spread(*spreads[stage]))
        for copy in group:
            copy.wait_recv()
        squares = sums[stage, 0]
        for k in range(1, size):
            squares = squares + sums[stage, k]
    total[...] = jnp.broadcast_to(jnp.sum(squares), total.shape)
    for copy in back[-1]:
        copy.wait_recv()
    for copy in list(copies.values()) + stage0 + stage1 + stage2 + [stage3] + norm_copies + sum(back, []):
        copy.wait_send()


def move_kernel(
    limit,
    grad,
    total,
    master,
    first,
    second,
    partner,
    weight,
    rest,
    high_out,
    high_in,
    high_to,
    rest_out,
    rest_in,
    rest_to,
    ssem,
    rsem,
    a_ssem,
    a_rsem,
):
    zl, x, e = (lax.axis_index(a) for a in ALL)
    rows, wide = grad.shape
    half = wide // 2
    tall = rows + 16

    def peer(j):
        return {"e": (e + j) % GROUPS}

    def at_x(j):
        return {"x": (x + j) % 4}

    pair = {"zl": 1 - zl}

    barrier = pltpu.get_barrier_semaphore()

    def greet(j, carry):
        pl.semaphore_signal(barrier, inc=1, device_id=peer(j), device_id_type=MESH)
        return carry

    lax.fori_loop(1, GROUPS, greet, 0)
    for device in (at_x(1), at_x(3), pair):
        pl.semaphore_signal(barrier, inc=1, device_id=device, device_id_type=MESH)

    factor = jnp.minimum(1.0, limit / (jnp.sqrt(total[0:1, 0:1]) + norm_eps))

    @pl.loop(0, GROUPS)
    def _(g):
        cols = pl.ds(pl.multiple_of(g * LANES, LANES), LANES)
        gradient = factor * grad[:, cols]
        first_new = beta_first * first[:, cols] + (1.0 - beta_first) * gradient
        second_new = beta_second * second[:, cols] + (1.0 - beta_second) * gradient * gradient
        ratio = first_new / correct_first / (jnp.sqrt(second_new / correct_second) + adam_eps)
        weights = master[:, cols]
        master_new = weights - learn_rate * (ratio + decay_weight * weights)
        high = master_new.astype(jnp.bfloat16)
        high_out[g] = high
        for k, values in enumerate((master_new - high.astype(F32), first_new, second_new)):
            code = code_of(jnp.max(jnp.abs(values), axis=0, keepdims=True))
            rest_out[g, k * tall : k * tall + rows, :] = to_codes(values, code)
            rest_out[g, k * tall + rows : (k + 1) * tall, :] = jnp.broadcast_to(code, (16, LANES)).astype(I16)

    pl.semaphore_wait(barrier, GROUPS + 2)

    def out_copy(src, dst, k, j):
        return pltpu.make_async_remote_copy(
            src_ref=src.at[(e + j) % GROUPS],
            dst_ref=dst.at[j],
            send_sem=ssem.at[k, j],
            recv_sem=rsem.at[k, j],
            device_id=peer(j),
            device_id_type=MESH,
        )

    my_rows = (zl * 4 + x) * rows

    def weight_part(block, col, width):
        return weight.at[
            pl.ds(pl.multiple_of(block * rows, 16), rows), pl.ds(pl.multiple_of(col, LANES), width)
        ]

    def back_copy(k, j):
        if k == 2:
            src, dst = high_to.at[(e + j) % GROUPS], weight_part(zl * 4 + x, e * LANES, LANES)
        else:
            src, dst = rest_to.at[(e + j) % GROUPS], rest.at[:, pl.ds(pl.multiple_of(e * LANES, LANES), LANES)]
        return pltpu.make_async_remote_copy(
            src_ref=src,
            dst_ref=dst,
            send_sem=ssem.at[k, j],
            recv_sem=rsem.at[k, j],
            device_id=peer(j),
            device_id_type=MESH,
        )

    def each(act):
        def step(j, carry):
            act(j)
            return carry

        lax.fori_loop(1, GROUPS, step, 0)

    def permute(own, arrived, to):
        def step(p, carry):
            distance = (e - partner[p] + GROUPS) % GROUPS
            to[p] = arrived[distance]
            return carry

        arrived[0] = own[e]
        lax.fori_loop(0, GROUPS, step, 0)

    each(lambda j: out_copy(high_out, high_in, 0, j).start())
    each(lambda j: out_copy(high_out, high_in, 0, j).wait_recv())
    permute(high_out, high_in, high_to)
    each(lambda j: back_copy(2, j).start())
    mine = pl.ds(pl.multiple_of(e * LANES, LANES), LANES)
    weight[pl.ds(pl.multiple_of(my_rows, 16), rows), mine] = high_to[e]
    each(lambda j: out_copy(rest_out, rest_in, 1, j).start())
    each(lambda j: back_copy(2, j).wait_recv())

    def gather(n, block, col, width, device):
        part = weight_part(block, col, width)
        return send(part, part, a_ssem.at[n], a_rsem.at[n], device)

    own, twin = zl * 4 + x, (1 - zl) * 4 + x
    left, right = (x + 3) % 4, (x + 1) % 4
    g_pair = gather(0, own, 0, wide, pair)
    g_right = gather(1, own, 0, wide, at_x(1))
    g_left = gather(2, own, 0, wide, at_x(3))

    g_pair.wait_recv()
    t_right = gather(3, twin, 0, wide, at_x(1))
    t_left = gather(4, twin, 0, wide, at_x(3))
    g_right.wait_recv()
    f_right = gather(5, zl * 4 + left, 0, half, at_x(1))
    g_left.wait_recv()
    f_left = gather(6, zl * 4 + right, half, half, at_x(3))

    each(lambda j: out_copy(rest_out, rest_in, 1, j).wait_recv())
    permute(rest_out, rest_in, rest_to)
    each(lambda j: back_copy(3, j).start())
    rest[:, mine] = rest_to[e]

    t_right.wait_recv()
    h_right = gather(7, (1 - zl) * 4 + left, 0, half, at_x(1))
    t_left.wait_recv()
    h_left = gather(8, (1 - zl) * 4 + right, half, half, at_x(3))
    each(lambda j: back_copy(3, j).wait_recv())
    for copy in (f_right, f_left, h_right, h_left):
        copy.wait_recv()
    each(lambda j: out_copy(high_out, high_in, 0, j).wait_send())
    each(lambda j: out_copy(rest_out, rest_in, 1, j).wait_send())
    each(lambda j: back_copy(2, j).wait_send())
    each(lambda j: back_copy(3, j).wait_send())
    for copy in (g_pair, g_right, g_left, t_right, t_left, f_right, f_left, h_right, h_left):
        copy.wait_send()


def adam_update(gradient, moment_one, moment_two, weights):
    first_new = beta_first * moment_one + (1.0 - beta_first) * gradient
    second_new = beta_second * moment_two + (1.0 - beta_second) * gradient * gradient
    ratio = first_new / correct_first / (jnp.sqrt(second_new / correct_second) + adam_eps)
    weights_new = weights - learn_rate * (ratio + decay_weight * weights)
    return (weights_new, first_new, second_new)


def on_device(
    hidden,
    upstream,
    token_counts,
    master,
    first_moment,
    second_moment,
    router_input,
    router_cot,
    router_master,
    router_first,
    router_second,
    partner,
):
    depth, units = hidden.shape[1:]
    wide = upstream.shape[2]
    rows = units // 8
    n_router = router_cot.shape[0]
    vmem = pl.BlockSpec(memory_space=pltpu.VMEM)
    smem = pl.BlockSpec(memory_space=pltpu.SMEM)
    dma = pltpu.SemaphoreType.DMA
    coded = wide + LANES
    r_rows, r_cols = n_router // 4, wide // 4
    gradient, router_grad, total = pl.pallas_call(
        reduce_kernel,
        out_shape=(
            jax.ShapeDtypeStruct((rows, wide), F32),
            jax.ShapeDtypeStruct((n_router, wide), F32),
            jax.ShapeDtypeStruct((8, LANES), F32),
        ),
        in_specs=[vmem, vmem, smem, vmem, vmem],
        out_specs=(vmem, vmem, vmem),
        scratch_shapes=[
            pltpu.VMEM((units, depth), jnp.bfloat16),
            pltpu.VMEM((rows, wide), F32),
            pltpu.VMEM((4, rows, wide), F32),
            pltpu.VMEM((7, rows, coded), I16),
            pltpu.VMEM((7, rows, coded), I16),
            pltpu.VMEM((n_router, wide), F32),
            pltpu.VMEM((3, r_rows, wide), F32),
            pltpu.VMEM((r_rows, wide), F32),
            pltpu.VMEM((3, r_rows, r_cols), F32),
            pltpu.VMEM((r_rows, r_cols), F32),
            pltpu.VMEM((3, r_rows, LANES), F32),
            pltpu.VMEM((r_rows, LANES), F32),
            pltpu.VMEM((8, LANES), F32),
            pltpu.VMEM((4, 4, 8, LANES), F32),
            dma((7, 2)),
            dma((7, 2)),
            dma((8, 4)),
            dma((8, 4)),
            dma((4, 4)),
            dma((4, 4)),
        ],
        compiler_params=pltpu.CompilerParams(
            collective_id=0, has_side_effects=True, vmem_limit_bytes=60 * 1024 * 1024
        ),
        name="reduce",
    )(hidden[0], upstream[0], token_counts, router_cot, router_input)

    clip_limit = 2.0 * math.sqrt(float(GROUPS * units * wide + n_router * wide))
    tall = rows + 16
    weight, rest = pl.pallas_call(
        functools.partial(move_kernel, clip_limit),
        out_shape=(
            jax.ShapeDtypeStruct((units, wide), jnp.bfloat16),
            jax.ShapeDtypeStruct((3 * tall, wide), I16),
        ),
        in_specs=[vmem, vmem, vmem, vmem, vmem, smem],
        out_specs=(vmem, vmem),
        scratch_shapes=[
            *[pltpu.VMEM((GROUPS, rows, LANES), jnp.bfloat16)] * 3,
            *[pltpu.VMEM((GROUPS, 3 * tall, LANES), I16)] * 3,
            dma((4, GROUPS)),
            dma((4, GROUPS)),
            dma((9,)),
            dma((9,)),
        ],
        compiler_params=pltpu.CompilerParams(
            collective_id=1, has_side_effects=True, vmem_limit_bytes=60 * 1024 * 1024
        ),
        name="move",
    )(gradient, total, master[0], first_moment[0], second_moment[0], partner)

    factor = jnp.minimum(1.0, clip_limit / (jnp.sqrt(total[0, 0]) + norm_eps))
    router_outs = adam_update(factor * router_grad, router_first, router_second, router_master)

    def decoded(k):
        codes = rest[k * tall : k * tall + rows].astype(F32)
        return codes * scale_of(rest[k * tall + rows : k * tall + rows + 1].astype(F32))

    own = lax.axis_index("zl") * 4 + lax.axis_index("x")
    high = lax.dynamic_slice_in_dim(weight, own * rows, rows, 0)
    new_master = high.astype(F32) + decoded(0)
    return (
        weight[None],
        new_master[None],
        decoded(1)[None],
        decoded(2)[None],
        router_outs[0],
        router_outs[1],
        router_outs[2],
    )


def solution(mesh):
    split = Mesh(mesh.devices.reshape(2, 4, mesh.shape["expert"]), ALL)
    return jax.shard_map(
        on_device,
        mesh=split,
        in_specs=(
            P("e", DP, None),
            P("e", DP, None),
            P("e", DP),
            P("e", DP, None),
            P("e", DP, None),
            P("e", DP, None),
            P(ALL, None),
            P(None, ALL),
            P(),
            P(),
            P(),
            P(),
        ),
        out_specs=(
            P("e", None, None),
            P("e", DP, None),
            P("e", DP, None),
            P("e", DP, None),
            P(),
            P(),
            P(),
        ),
        check_vma=False,
    )
```

time: 539 us -> 220 us (0.41)
  the two profiles are of different devices: /device:TPU:1 before, /device:TPU:81 now
where the time goes in v1:
time: 220 us
  Pallas kernels  208 us (95%)
  other arithmetic  6.63 us (3%)
  local copies, waits for them, and re-layouts  3.75 us (2%)
    pallas_call x1, Pallas kernels, on_device(): pl.pallas_call(functools.partial(move_kernel, clip_limit), out_shape=(jax...  118 us
    pallas_call x1, Pallas kernels, on_device(): pl.pallas_call(reduce_kernel, out_shape=(jax.ShapeDtypeStruct((rows, wide...  89.2 us

profile of v1, /device:TPU:81, one launch (start us, length us, event | category | flops | bytes accessed | tf_op | source)
XLA Modules:
  0.0 220.1 jit_solution(7060484126400930033)
XLA Ops:
  1.3 89.2 %reduce.1 = (f32[176,2048]{1,0:T(8,128)}, f32[64,2048]{1,0:T(8,128)}, f32[8,128]{1,0:T(8,128)}) custom-call(bf16[1152,1408]{1,0:T(8,128)(2,1)} %bitcast.18, bf16[1152,2048]{1,0:T(8,128)(2,1)} %bitcast.17, s32[1,1]{1,0:T(1,128)S(6)} %copy.20.counts, bf16[64,128]{1,0:T(8,128)(2,1)} %cot.1, bf16[128,2048]{1,0:T(8,128)(2,1)} %rin.1), custom_call_target="tpu_custom_call" | custom-call | tf_op jit(solution)/shard_map/reduce/pallas_call | solution.py:496
  90.5 0.0 copy-start.3
  90.5 0.0 copy-start.4
  90.5 118.5 %move.1 = (bf16[1408,2048]{1,0:T(8,128)(2,1)}, s16[576,2048]{1,0:T(8,128)(2,1)}) custom-call(f32[176,2048]{1,0:T(8,128)} %get-tuple-element.12.grad, f32[8,128]{1,0:T(8,128)} %get-tuple-element.13.total, f32[176,2048]{1,0:T(8,128)} %bitcast.19, f32[176,2048]{1,0:T(8,128)} %bitcast.20, f32[176,2048]{1,0:T(8,128)} %bitcast.21, s32[16]{0:T(128)} %partner.1), custom_call_target="tpu_custom_call" | custom-call | tf_op jit(solution)/shard_map/move/pallas_call | solution.py:535
  209.0 0.9 multiply_exponential_fusion
  209.8 0.0 copy-start.1
  209.8 0.0 copy-start.2
  209.9 0.0 copy-start
  209.9 4.4 %multiply_bitcast_fusion = (f32[1,176,2048]{2,1,0:T(8,128)}, f32[1,176,2048]{2,1,0:T(8,128)}, f32[1,176,2048]{2,1,0:T(8,128)}) fusion(f32[2048]{0:T(1024)S(1)} %bitcast.22, s16[576,2048]{1,0:T(8,128)(2,1)} %get-tuple-element.15, f32[2048]{0:T(1024)S(1)} %bitcast.23, f32[2048]{0:T(1024)S(1)} %bitcast.24, bf16[1408,2048]{1,0:T(8,128)(2,1)} %get-tuple-element.14, ...), kind=kLoop, calls=%fused_computation | loop fusion | flops 2883584 | bytes 7233540 | tf_op jit(solution)/shard_map/broadcast_in_dim | solution.py:571
  214.2 1.2 slice.27
  216.1 0.0 copy-done.3
  216.2 0.0 copy-done.4
  216.2 0.0 copy-done.1
  216.2 0.0 copy-done.2
  216.2 1.4 multiply_subtract_fusion
  217.6 0.0 copy-done
  217.6 2.5 %copy.21 = bf16[1,1408,2048]{2,1,0:T(8,128)(2,1)} copy(bf16[1,1408,2048]{2,1,0:T(8,128)(2,1)S(1)} %bitcast.16) | data formatting | bytes 11534336
Async XLA Ops:
  90.5 125.7 %copy-start.3 = (f32[64,2048]{1,0:T(8,128)S(1)}, f32[64,2048]{1,0:T(8,128)}, u32[]{:S(2)}) copy-start(f32[64,2048]{1,0:T(8,128)} %param.22) | copy-start | bytes 1572868
  90.5 125.7 %copy-start.4 = (f32[64,2048]{1,0:T(8,128)S(1)}, f32[64,2048]{1,0:T(8,128)}, u32[]{:S(2)}) copy-start(f32[64,2048]{1,0:T(8,128)} %get-tuple-element.16) | copy-start | bytes 1572868
  209.8 6.3 %copy-start.1 = (f32[64,2048]{1,0:T(8,128)S(1)}, f32[64,2048]{1,0:T(8,128)}, u32[]{:S(2)}) copy-start(f32[64,2048]{1,0:T(8,128)} %param.20) | copy-start | bytes 1572868
  209.8 6.3 %copy-start.2 = (f32[64,2048]{1,0:T(8,128)S(1)}, f32[64,2048]{1,0:T(8,128)}, u32[]{:S(2)}) copy-start(f32[64,2048]{1,0:T(8,128)} %param.21) | copy-start | bytes 1572868
  209.9 7.8 %copy-start = (bf16[1408,2048]{1,0:T(8,128)(2,1)S(1)}, bf16[1408,2048]{1,0:T(8,128)(2,1)}, u32[]{:S(2)}) copy-start(bf16[1408,2048]{1,0:T(8,128)(2,1)} %get-tuple-element.14) | copy-start | bytes 17301508

commit v2 on v1

v2 whole, which is shorter than its diff:
```python
import functools
import math

import jax
import jax.numpy as jnp
from jax import lax
from jax.experimental import pallas as pl
from jax.experimental.pallas import tpu as pltpu
from jax.sharding import Mesh
from jax.sharding import PartitionSpec as P

MESH = pl.DeviceIdType.MESH
DP = ("zl", "x")
ALL = ("zl", "x", "e")
F32 = jnp.float32
I16 = jnp.int16

beta_first = 0.9
beta_second = 0.95
learn_rate = 0.001
decay_weight = 0.1
adam_eps = 1e-08
norm_eps = 1e-06
correct_first = 1.0 - 0.9**10
correct_second = 1.0 - 0.95**10

GROUPS = 16
LANES = 128
TOP = 15.0
SMALL = 2.0**-100


def code_of(peak):
    return jnp.ceil(16.0 * jnp.log2(jnp.maximum(peak, SMALL)))


def to_codes(values, code):
    scaled = jnp.round(values * jnp.exp2(TOP - code * (1.0 / 16.0)))
    return jnp.clip(scaled, -32767.0, 32767.0).astype(I16)


def scale_of(code):
    return jnp.exp2(code * (1.0 / 16.0) - TOP)


def encode_rows(values, dst, rows):
    width = values.shape[1]
    code = code_of(jnp.max(jnp.abs(values), axis=1, keepdims=True))
    dst[rows, :width] = to_codes(values, code)
    dst[rows, width:] = jnp.broadcast_to(code, (values.shape[0], LANES)).astype(I16)


def decode_rows(src, rows, width):
    code = src[rows, width : width + LANES].astype(F32)[:, :1]
    return src[rows, :width].astype(F32) * scale_of(code)


def send(src, dst, send_sem, recv_sem, device):
    copy = pltpu.make_async_remote_copy(
        src_ref=src, dst_ref=dst, send_sem=send_sem, recv_sem=recv_sem, device_id=device, device_id_type=MESH
    )
    copy.start()
    return copy


def reduce_kernel(
    hid,
    up,
    counts,
    cot,
    rin,
    grad,
    rgrad,
    total,
    hid_t,
    terms,
    x_out,
    x_in,
    late_out,
    late_in,
    z_out,
    z_in,
    last_out,
    last_in,
    rp,
    r_in0,
    r1,
    r_in1,
    r2,
    r_in2,
    r3,
    r_in3,
    sums,
    x_ssem,
    x_rsem,
    z_ssem,
    z_rsem,
    r_ssem,
    r_rsem,
    n_ssem,
    n_rsem,
):
    zl, x, e = (lax.axis_index(a) for a in ALL)
    y, zh, core = e // 4, (e // 2) % 2, e % 2
    z = zh * 2 + zl
    depth, units = hid.shape
    wide = up.shape[1]
    rows = units // 8
    early = x_out.shape[1]
    late = rows - early
    late_a = late_out.shape[1]
    late_b = late - late_a

    def at_x(j):
        return {"x": (x + j) % 4}

    def at_z(j):
        there = (z + j) % 4
        return {"zl": there % 2, "e": y * 4 + (there // 2) * 2 + core}

    def at_y(j):
        return {"e": ((y + j) % 4) * 4 + zh * 2 + core}

    def at_core(j):
        return {"e": e + 1 - 2 * core}

    pair = {"zl": 1 - zl}
    axes = ((at_x, 4, x), (at_z, 4, z), (at_y, 4, y), (at_core, 2, core))

    barrier = pltpu.get_barrier_semaphore()
    for at, size, _ in axes:
        for j in range(1, size):
            pl.semaphore_signal(barrier, inc=1, device_id=at(j), device_id_type=MESH)

    live = counts[0, 0]
    keep = (lax.broadcasted_iota(jnp.int32, (depth, LANES), 0) < live).astype(F32).astype(jnp.bfloat16)

    @pl.loop(0, units // LANES)
    def _(t):
        cols = pl.ds(pl.multiple_of(t * LANES, LANES), LANES)
        hid_t[cols, :] = (hid[:, cols] * keep).T

    def multiply(block):
        at = pl.multiple_of(block * rows, 16)

        @pl.loop(0, wide // 512)
        def _(n):
            cols = pl.ds(pl.multiple_of(n * 512, 512), 512)
            terms[block, :, cols] = jnp.dot(hid_t[pl.ds(at, rows), :], up[:, cols], preferred_element_type=F32)

    def tiles(start, size, act):
        @pl.loop(0, size // 16, unroll=True)
        def _(i):
            act(
                pl.ds(pl.multiple_of(start + i * 16, 16), 16),
                pl.ds(pl.multiple_of(i * 16, 16), 16),
            )

    def x_copy(slot, device):
        return send(x_out.at[slot], x_in.at[slot], x_ssem.at[slot], x_rsem.at[slot], device)

    def late_copy(slot, size, device):
        r = pl.ds(0, size)
        return send(
            late_out.at[slot, r], late_in.at[slot, r], x_ssem.at[6 + slot], x_rsem.at[6 + slot], device
        )

    def early_part(block, slot, step, incoming=None):
        def act(r, i):
            values = terms[block, r, :]
            if incoming is not None:
                values = values + decode_rows(x_in.at[incoming], i, wide)
            encode_rows(values, x_out.at[slot], i)

        tiles(0, early, act)
        return x_copy(slot, at_x(step))

    def pair_part(n, there):
        def act(r, i):
            encode_rows(terms[(1 - zl) * 4 + there, r, :], z_out.at[n], i)

        tiles(early, late, act)
        return send(z_out.at[n], z_in.at[n], z_ssem.at[n], z_rsem.at[n], pair)

    def pair_sum(n, there):
        block = zl * 4 + there

        def act(r, i):
            terms[block, r, :] += decode_rows(z_in.at[n], i, wide)

        tiles(early, late, act)

    def late_part(there, start, size, slot, step, incoming=None):
        block = zl * 4 + there

        def act(r, i):
            values = terms[block, r, :]
            if incoming is not None:
                values = values + decode_rows(late_in.at[incoming], i, wide)
            encode_rows(values, late_out.at[slot], i)

        tiles(start, size, act)
        return late_copy(slot, size, at_x(step))

    far, right, left = (x + 2) % 4, (x + 1) % 4, (x + 3) % 4
    a_at, b_at = early, early + late_a

    multiply(far)
    pl.semaphore_wait(barrier, 10)
    e0 = early_part(far, 0, 3)
    multiply(4 + far)
    e1 = early_part(4 + far, 1, 1)
    p0 = pair_part(0, far)
    multiply(right)
    e2 = early_part(right, 2, 1)
    multiply(4 + left)
    e3 = early_part(4 + left, 3, 3)
    multiply(4 + right)
    p1 = pair_part(1, right)

    rp[...] = jnp.dot(cot[...], rin[...], preferred_element_type=F32)
    n_router = rp.shape[0]
    r_half, r_cols = n_router // 2, wide // 4
    s0 = send(
        rp.at[pl.ds(pl.multiple_of((1 - core) * r_half, 8), r_half)],
        r_in0,
        r_ssem.at[0, 1],
        r_rsem.at[0, 1],
        at_core(1),
    )
    multiply(left)
    p2 = pair_part(2, left)
    s0.wait_recv()
    r1[...] = rp[pl.ds(pl.multiple_of(core * r_half, 8), r_half), :] + r_in0[...]
    s1 = [
        send(
            r1.at[pl.ds(pl.multiple_of(((y + j) % 4) * 8, 8), 8)],
            r_in1.at[j - 1],
            r_ssem.at[1, j],
            r_rsem.at[1, j],
            at_y(j),
        )
        for j in range(1, 4)
    ]
    multiply(x)
    multiply(4 + x)
    p3 = pair_part(3, x)

    e0.wait_recv()
    e4 = early_part(left, 4, 3, 0)
    e1.wait_recv()
    e5 = early_part(4 + right, 5, 1, 1)
    p0.wait_recv()
    pair_sum(0, far)
    l0 = late_part(far, a_at, late_a, 0, 3)
    l1 = late_part(far, b_at, late_b, 1, 1)

    for copy in s1:
        copy.wait_recv()
    r2[...] = r1[pl.ds(pl.multiple_of(y * 8, 8), 8), :] + r_in1[0] + r_in1[1] + r_in1[2]
    s2 = [
        send(
            r2.at[:, pl.ds(pl.multiple_of(((z + j) % 4) * r_cols, LANES), r_cols)],
            r_in2.at[j - 1],
            r_ssem.at[2, j],
            r_rsem.at[2, j],
            at_z(j),
        )
        for j in range(1, 4)
    ]
    p1.wait_recv()
    pair_sum(1, right)
    l2 = late_part(right, a_at, late_a, 2, 1)
    p2.wait_recv()
    pair_sum(2, left)
    l3 = late_part(left, b_at, late_b, 3, 3)

    for copy in (e2, e3, e4, e5):
        copy.wait_recv()

    def fold(r, i):
        terms[x, r, :] += decode_rows(x_in.at[2], i, wide) + decode_rows(x_in.at[4], i, wide)
        terms[4 + x, r, :] += decode_rows(x_in.at[3], i, wide) + decode_rows(x_in.at[5], i, wide)
        encode_rows(terms[(1 - zl) * 4 + x, r, :], last_out, i)

    tiles(0, early, fold)
    last = send(last_out, last_in, z_ssem.at[4], z_rsem.at[4], pair)

    l0.wait_recv()
    l4 = late_part(left, a_at, late_a, 4, 3, 0)
    l1.wait_recv()
    l5 = late_part(right, b_at, late_b, 5, 1, 1)
    p3.wait_recv()
    pair_sum(3, x)

    for copy in s2:
        copy.wait_recv()
    r3[...] = r2[:, pl.ds(pl.multiple_of(z * r_cols, LANES), r_cols)] + r_in2[0] + r_in2[1] + r_in2[2]
    s3 = [
        send(
            r3.at[:, pl.ds(pl.multiple_of(((x + j) % 4) * LANES, LANES), LANES)],
            r_in3.at[j - 1],
            r_ssem.at[3, j],
            r_rsem.at[3, j],
            at_x(j),
        )
        for j in range(1, 4)
    ]

    own = zl * 4 + x

    def count(values, acc):
        values = values * values
        for a in range(2):
            for b in range(wide // LANES):
                acc = acc + values[a * 8 : a * 8 + 8, b * LANES : (b + 1) * LANES]
        return acc

    def close(start, size, acc, sources):
        def step(n, acc):
            i = pl.ds(pl.multiple_of(n * 16, 16), 16)
            r = pl.ds(pl.multiple_of(start + n * 16, 16), 16)
            values = terms[own, r, :]
            for source in sources:
                values = values + decode_rows(source, i, wide)
            grad[r, :] = values
            return count(values, acc)

        return lax.fori_loop(0, size // 16, step, acc, unroll=True)

    squares = jnp.zeros((8, LANES), F32)
    last.wait_recv()
    squares = close(0, early, squares, (last_in,))
    for copy in (l2, l4):
        copy.wait_recv()
    squares = close(a_at, late_a, squares, (late_in.at[2], late_in.at[4]))
    for copy in (l3, l5):
        copy.wait_recv()
    squares = close(b_at, late_b, squares, (late_in.at[3], late_in.at[5]))

    for copy in s3:
        copy.wait_recv()
    piece = r3[:, pl.ds(pl.multiple_of(x * LANES, LANES), LANES)] + r_in3[0] + r_in3[1] + r_in3[2]
    squares = squares + piece * piece
    my_row = core * r_half + y * 8
    z_col = z * r_cols
    x_col = z_col + x * LANES
    rgrad[pl.ds(pl.multiple_of(my_row, 8), 8), pl.ds(pl.multiple_of(x_col, LANES), LANES)] = piece

    waits = [e0, e1, e2, e3, e4, e5, l0, l1, l2, l3, l4, l5, p0, p1, p2, p3, last, s0, *s1, *s2, *s3]
    spread = (
        (my_row, 8, x_col, LANES),
        (my_row, 8, z_col, r_cols),
        (my_row, 8, 0, wide),
        (core * r_half, r_half, 0, wide),
    )
    back = []
    for stage, (at, size, here) in enumerate(axes):
        sums[stage, here] = squares
        mine = sums.at[stage, here]
        group = [
            send(mine, mine, n_ssem.at[stage, j], n_rsem.at[stage, j], at(j)) for j in range(1, size)
        ]
        for copy in back:
            copy.wait_recv()
        row, height, col, width = spread[stage]
        part = rgrad.at[pl.ds(pl.multiple_of(row, 8), height), pl.ds(pl.multiple_of(col, LANES), width)]
        back = [
            send(part, part, r_ssem.at[4 + stage, j], r_rsem.at[4 + stage, j], at(j)) for j in range(1, size)
        ]
        waits += group + back
        for copy in group:
            copy.wait_recv()
        squares = sums[stage, 0]
        for k in range(1, size):
            squares = squares + sums[stage, k]
    total[...] = jnp.broadcast_to(jnp.sum(squares), total.shape)
    for copy in back:
        copy.wait_recv()
    for copy in waits:
        copy.wait_send()


def adam_update(gradient, moment_one, moment_two, weights):
    first_new = beta_first * moment_one + (1.0 - beta_first) * gradient
    second_new = beta_second * moment_two + (1.0 - beta_second) * gradient * gradient
    ratio = first_new / correct_first / (jnp.sqrt(second_new / correct_second) + adam_eps)
    weights_new = weights - learn_rate * (ratio + decay_weight * weights)
    return (weights_new, first_new, second_new)


def each(act, start=1):
    def step(j, carry):
        act(j)
        return carry

    lax.fori_loop(start, GROUPS, step, 0)


def move_kernel(
    limit,
    grad,
    total,
    master,
    first,
    second,
    partner,
    weight,
    new_master,
    new_first,
    new_second,
    leaving,
    middle0,
    middle1,
    middle2,
    turned,
    landed,
    ssem,
    rsem,
    a_ssem,
    a_rsem,
):
    zl, x, e = (lax.axis_index(a) for a in ALL)
    rows, wide = grad.shape
    half = wide // 2
    results = (new_master, new_first, new_second)
    middle = (middle0, middle1, middle2)

    def peer(j):
        return {"e": (e + j) % GROUPS}

    def at_x(j):
        return {"x": (x + j) % 4}

    pair = {"zl": 1 - zl}

    barrier = pltpu.get_barrier_semaphore()
    each(lambda j: pl.semaphore_signal(barrier, inc=1, device_id=peer(j), device_id_type=MESH))
    for device in (at_x(1), at_x(3), pair):
        pl.semaphore_signal(barrier, inc=1, device_id=device, device_id_type=MESH)

    factor = jnp.minimum(1.0, limit / (jnp.sqrt(total[0:1, 0:1]) + norm_eps))

    def columns(g):
        return pl.ds(pl.multiple_of(g * LANES, LANES), LANES)

    def update(g):
        c = columns(g)
        return adam_update(factor * grad[:, c], first[:, c], second[:, c], master[:, c])

    def encode(k, g, values):
        code = code_of(jnp.max(jnp.abs(values), axis=0, keepdims=True))
        leaving[k, g, 0:rows, :] = to_codes(values, code)
        leaving[k, g, rows:, :] = jnp.broadcast_to(code, (16, LANES)).astype(I16)

    def decode(k, g):
        piece = landed.at[k, g]
        values = piece[0:rows, :].astype(F32) * scale_of(piece[rows : rows + 1, :].astype(F32))
        results[k][:, columns(g)] = values
        return values

    def remote(src, dst, phase, k, j):
        return pltpu.make_async_remote_copy(
            src_ref=src,
            dst_ref=dst,
            send_sem=ssem.at[phase, k, j],
            recv_sem=rsem.at[phase, k, j],
            device_id=peer(j),
            device_id_type=MESH,
        )

    def go(k, j):
        return remote(leaving.at[k, (e + j) % GROUPS], middle[k].at[j], 0, k, j)

    def come(k, j):
        return remote(turned.at[k, (e + j) % GROUPS], landed.at[k, e], 1, k, j)

    def permute(k):
        middle[k][0] = leaving[k, e]

        def step(p, carry):
            turned[k, p] = middle[k][(e - partner[p] + GROUPS) % GROUPS]
            return carry

        lax.fori_loop(0, GROUPS, step, 0)

    def turn(k):
        each(lambda j: go(k, j).wait_recv())
        permute(k)
        each(lambda j: come(k, j).start())
        landed[k, e] = turned[k, e]

    encode(0, e, update(e)[0])
    pl.semaphore_wait(barrier, GROUPS + 2)

    def first_leg(j):
        g = (e + j) % GROUPS
        encode(0, g, update(g)[0])
        go(0, j).start()

    each(first_leg)

    def moments(g):
        _, first_new, second_new = update(g)
        encode(1, g, first_new)
        encode(2, g, second_new)

    each(moments, 0)
    turn(0)

    def weight_part(block, col, width):
        return weight.at[
            pl.ds(pl.multiple_of(block * rows, 16), rows), pl.ds(pl.multiple_of(col, LANES), width)
        ]

    own, twin = zl * 4 + x, (1 - zl) * 4 + x
    own_rows = pl.ds(pl.multiple_of(own * rows, 16), rows)

    def settle(g):
        weight[own_rows, columns(g)] = decode(0, g).astype(jnp.bfloat16)

    settle(e)

    def settle_next(j):
        come(0, j).wait_recv()
        settle((e - j + GROUPS) % GROUPS)

    each(settle_next)

    def gather(n, block, col, width, device):
        part = weight_part(block, col, width)
        return send(part, part, a_ssem.at[n], a_rsem.at[n], device)

    left, right = (x + 3) % 4, (x + 1) % 4
    g_pair = gather(0, own, 0, wide, pair)
    g_right = gather(1, own, 0, wide, at_x(1))
    g_left = gather(2, own, 0, wide, at_x(3))
    each(lambda j: go(1, j).start())
    each(lambda j: go(2, j).start())

    g_pair.wait_recv()
    t_right = gather(3, twin, 0, wide, at_x(1))
    t_left = gather(4, twin, 0, wide, at_x(3))
    g_right.wait_recv()
    f_right = gather(5, zl * 4 + left, 0, half, at_x(1))
    g_left.wait_recv()
    f_left = gather(6, zl * 4 + right, half, half, at_x(3))

    turn(1)
    t_right.wait_recv()
    h_right = gather(7, (1 - zl) * 4 + left, 0, half, at_x(1))
    t_left.wait_recv()
    h_left = gather(8, (1 - zl) * 4 + right, half, half, at_x(3))
    turn(2)

    for k in (1, 2):
        decode(k, e)

        def finish(j, k=k):
            come(k, j).wait_recv()
            decode(k, (e - j + GROUPS) % GROUPS)

        each(finish)
    for copy in (f_right, f_left, h_right, h_left):
        copy.wait_recv()
    for k in range(3):
        each(lambda j, k=k: go(k, j).wait_send())
        each(lambda j, k=k: come(k, j).wait_send())
    for copy in (g_pair, g_right, g_left, t_right, t_left, f_right, f_left, h_right, h_left):
        copy.wait_send()


def on_device(
    hidden,
    upstream,
    token_counts,
    master,
    first_moment,
    second_moment,
    router_input,
    router_cot,
    router_master,
    router_first,
    router_second,
    partner,
):
    depth, units = hidden.shape[1:]
    wide = upstream.shape[2]
    rows = units // 8
    n_router = router_cot.shape[0]
    vmem = pl.BlockSpec(memory_space=pltpu.VMEM)
    smem = pl.BlockSpec(memory_space=pltpu.SMEM)
    dma = pltpu.SemaphoreType.DMA
    coded = wide + LANES
    r_half, r_cols = n_router // 2, wide // 4
    late = rows * 5 // 11 // 16 * 16
    early = rows - late
    late_a = (late // 16 + 1) // 2 * 16
    gradient, router_grad, total = pl.pallas_call(
        reduce_kernel,
        out_shape=(
            jax.ShapeDtypeStruct((rows, wide), F32),
            jax.ShapeDtypeStruct((n_router, wide), F32),
            jax.ShapeDtypeStruct((8, LANES), F32),
        ),
        in_specs=[vmem, vmem, smem, vmem, vmem],
        out_specs=(vmem, vmem, vmem),
        scratch_shapes=[
            pltpu.VMEM((units, depth), jnp.bfloat16),
            pltpu.VMEM((8, rows, wide), F32),
            *[pltpu.VMEM((6, early, coded), I16)] * 2,
            *[pltpu.VMEM((6, late_a, coded), I16)] * 2,
            *[pltpu.VMEM((4, late, coded), I16)] * 2,
            *[pltpu.VMEM((early, coded), I16)] * 2,
            pltpu.VMEM((n_router, wide), F32),
            pltpu.VMEM((r_half, wide), F32),
            pltpu.VMEM((r_half, wide), F32),
            pltpu.VMEM((3, 8, wide), F32),
            pltpu.VMEM((8, wide), F32),
            pltpu.VMEM((3, 8, r_cols), F32),
            pltpu.VMEM((8, r_cols), F32),
            pltpu.VMEM((3, 8, LANES), F32),
            pltpu.VMEM((4, 4, 8, LANES), F32),
            dma((12,)),
            dma((12,)),
            dma((5,)),
            dma((5,)),
            dma((8, 4)),
            dma((8, 4)),
            dma((4, 4)),
            dma((4, 4)),
        ],
        compiler_params=pltpu.CompilerParams(
            collective_id=0, has_side_effects=True, vmem_limit_bytes=40 * 1024 * 1024
        ),
        name="reduce",
    )(hidden[0], upstream[0], token_counts, router_cot, router_input)

    clip_limit = 2.0 * math.sqrt(float(GROUPS * units * wide + n_router * wide))
    tall = rows + 16
    state = jax.ShapeDtypeStruct((rows, wide), F32)
    weight, new_master, new_first, new_second = pl.pallas_call(
        functools.partial(move_kernel, clip_limit),
        out_shape=(jax.ShapeDtypeStruct((units, wide), jnp.bfloat16), state, state, state),
        in_specs=[vmem, vmem, vmem, vmem, vmem, smem],
        out_specs=(vmem, vmem, vmem, vmem),
        scratch_shapes=[
            pltpu.VMEM((3, GROUPS, tall, LANES), I16),
            *[pltpu.VMEM((GROUPS, tall, LANES), I16)] * 3,
            *[pltpu.VMEM((3, GROUPS, tall, LANES), I16)] * 2,
            dma((2, 3, GROUPS)),
            dma((2, 3, GROUPS)),
            dma((9,)),
            dma((9,)),
        ],
        compiler_params=pltpu.CompilerParams(
            collective_id=1, has_side_effects=True, vmem_limit_bytes=27 * 1024 * 1024
        ),
        name="move",
    )(gradient, total, master[0], first_moment[0], second_moment[0], partner)

    factor = jnp.minimum(1.0, clip_limit / (jnp.sqrt(total[0, 0]) + norm_eps))
    router_outs = adam_update(factor * router_grad, router_first, router_second, router_master)

    return (
        weight[None],
        new_master[None],
        new_first[None],
        new_second[None],
        router_outs[0],
        router_outs[1],
        router_outs[2],
    )


def solution(mesh):
    split = Mesh(mesh.devices.reshape(2, 4, mesh.shape["expert"]), ALL)
    return jax.shard_map(
        on_device,
        mesh=split,
        in_specs=(
            P("e", DP, None),
            P("e", DP, None),
            P("e", DP),
            P("e", DP, None),
            P("e", DP, None),
            P("e", DP, None),
            P(ALL, None),
            P(None, ALL),
            P(),
            P(),
            P(),
            P(),
        ),
        out_specs=(
            P("e", None, None),
            P("e", DP, None),
            P("e", DP, None),
            P("e", DP, None),
            P(),
            P(),
            P(),
        ),
        check_vma=False,
    )
```

time: 220 us -> 177 us (0.80)
  the two profiles are of different devices: /device:TPU:81 before, /device:TPU:1 now
where the time goes in v2:
time: 177 us
  Pallas kernels  161 us (91%)
  local copies, waits for them, and re-layouts  12.4 us (7%)
  between operations  2.13 us (1%)
    pallas_call x1, Pallas kernels, on_device(): pl.pallas_call(functools.partial(move_kernel, clip_limit), out_shape=(jax...  92 us
    pallas_call x1, Pallas kernels, on_device(): pl.pallas_call(reduce_kernel, out_shape=(jax.ShapeDtypeStruct((rows, wide...  68.8 us
    unnamed x26, local copies, waits for them, and re-layouts  11.9 us

profile of v2, /device:TPU:1, one launch (start us, length us, event | category | flops | bytes accessed | tf_op | source)
XLA Modules:
  0.0 176.7 jit_solution(9750310586163546208)
XLA Ops:
  1.3 0.0 copy-start
  1.3 2.3 %copy-done = bf16[1,1152,2048]{2,1,0:T(8,128)(2,1)S(1)} copy-done((bf16[1,1152,2048]{2,1,0:T(8,128)(2,1)S(1)}, bf16[1,1152,2048]{2,1,0:T(8,128)(2,1)}, u32[]{:S(2)}) %copy-start) | copy-done | bytes 4718616
  3.6 0.0 copy-start.1
  3.6 1.9 %copy-done.1 = bf16[1,1152,1408]{2,1,0:T(8,128)(2,1)S(1)} copy-done((bf16[1,1152,1408]{2,1,0:T(8,128)(2,1)S(1)}, bf16[1,1152,1408]{2,1,0:T(8,128)(2,1)}, u32[]{:S(2)}) %copy-start.1) | copy-done | bytes 3244056
  5.5 0.0 copy-start.5
  5.5 1.0 copy-done.5
  6.6 0.0 copy-start.6
  6.6 0.7 copy-done.6
  7.3 0.0 copy-start.2
  7.3 0.0 copy-start.3
  7.3 0.0 copy-start.4
  7.3 0.0 copy-start.7
  7.3 68.8 %reduce.1 = (f32[176,2048]{1,0:T(8,128)S(1)}, f32[64,2048]{1,0:T(8,128)S(1)}, f32[8,128]{1,0:T(8,128)S(1)}) custom-call(bf16[1152,1408]{1,0:T(8,128)(2,1)S(1)} %bitcast.12, bf16[1152,2048]{1,0:T(8,128)(2,1)S(1)} %bitcast.11, s32[1,1]{1,0:T(1,128)S(6)} %copy.23.counts, bf16[64,128]{1,0:T(8,128)(2,1)S(1)} %copy-done.6, bf16[128,2048]{1,0:T(8,128)(2,1)S(1)} %copy-done.5), custom_call_target="tpu_custom_call" | custom-call | tf_op jit(solution)/shard_map/reduce/pallas_call | solution.py:599
  76.1 0.0 copy-done.2
  76.2 0.0 copy-done.3
  76.2 0.0 copy-done.4
  76.2 0.0 copy-done.7
  76.2 0.0 copy-start.8
  76.2 0.0 copy-start.9
  76.2 0.0 copy-start.10
  76.2 92.0 %move.1 = (bf16[1408,2048]{1,0:T(8,128)(2,1)S(1)}, f32[176,2048]{1,0:T(8,128)S(1)}, f32[176,2048]{1,0:T(8,128)S(1)}, f32[176,2048]{1,0:T(8,128)S(1)}) custom-call(f32[176,2048]{1,0:T(8,128)S(1)} %get-tuple-element.14.grad, f32[8,128]{1,0:T(8,128)S(1)} %get-tuple-element.15.total, f32[176,2048]{1,0:T(8,128)S(1)} %bitcast.16, f32[176,2048]{1,0:T(8,128)S(1)} %bitcast.17, ...), custom_call_target="tpu_custom_call" | custom-call | tf_op jit(solution)/shard_map/move/pallas_call | solution.py:642
  168.2 0.5 slice.3
  169.5 0.0 copy-done.8
  169.5 0.0 copy-done.9
  169.5 0.0 copy-done.10
  169.5 1.4 multiply_subtract_fusion
  170.9 2.5 %copy.24 = bf16[1,1408,2048]{2,1,0:T(8,128)(2,1)} copy(bf16[1,1408,2048]{2,1,0:T(8,128)(2,1)S(1)} %bitcast.10) | data formatting | bytes 11534336
  173.4 1.1 copy.25
  174.5 1.1 copy.26
  175.6 1.1 copy.27
Async XLA Ops:
  1.3 2.3 %copy-start = (bf16[1,1152,2048]{2,1,0:T(8,128)(2,1)S(1)}, bf16[1,1152,2048]{2,1,0:T(8,128)(2,1)}, u32[]{:S(2)}) copy-start(bf16[1,1152,2048]{2,1,0:T(8,128)(2,1)} %param.13) | copy-start | bytes 14155780
  3.6 1.9 %copy-start.1 = (bf16[1,1152,1408]{2,1,0:T(8,128)(2,1)S(1)}, bf16[1,1152,1408]{2,1,0:T(8,128)(2,1)}, u32[]{:S(2)}) copy-start(bf16[1,1152,1408]{2,1,0:T(8,128)(2,1)} %param.12) | copy-start | bytes 9732100
  5.5 1.0 copy-start.5
  6.6 0.7 copy-start.6
  7.3 68.8 %copy-start.2 = (f32[1,176,2048]{2,1,0:T(8,128)S(1)}, f32[1,176,2048]{2,1,0:T(8,128)}, u32[]{:S(2)}) copy-start(f32[1,176,2048]{2,1,0:T(8,128)} %param.15) | copy-start | bytes 4325380
  7.3 68.9 %copy-start.3 = (f32[1,176,2048]{2,1,0:T(8,128)S(1)}, f32[1,176,2048]{2,1,0:T(8,128)}, u32[]{:S(2)}) copy-start(f32[1,176,2048]{2,1,0:T(8,128)} %param.16) | copy-start | bytes 4325380
  7.3 68.9 %copy-start.4 = (f32[1,176,2048]{2,1,0:T(8,128)S(1)}, f32[1,176,2048]{2,1,0:T(8,128)}, u32[]{:S(2)}) copy-start(f32[1,176,2048]{2,1,0:T(8,128)} %param.17) | copy-start | bytes 4325380
  7.3 68.9 %copy-start.7 = (s32[16]{0:T(128)S(1)}, s32[16]{0:T(128)}, u32[]{:S(2)}) copy-start(s32[16]{0:T(128)} %partner.1) | copy-start | bytes 196
  76.2 93.3 %copy-start.8 = (f32[64,2048]{1,0:T(8,128)S(1)}, f32[64,2048]{1,0:T(8,128)}, u32[]{:S(2)}) copy-start(f32[64,2048]{1,0:T(8,128)} %param.20) | copy-start | bytes 1572868
  76.2 93.3 %copy-start.9 = (f32[64,2048]{1,0:T(8,128)S(1)}, f32[64,2048]{1,0:T(8,128)}, u32[]{:S(2)}) copy-start(f32[64,2048]{1,0:T(8,128)} %param.21) | copy-start | bytes 1572868
  76.2 93.3 %copy-start.10 = (f32[64,2048]{1,0:T(8,128)S(1)}, f32[64,2048]{1,0:T(8,128)}, u32[]{:S(2)}) copy-start(f32[64,2048]{1,0:T(8,128)} %param.22) | copy-start | bytes 1572868

commit v3 on v2

--- a/solution.py
+++ b/solution.py
@@ -64,14 +64,18 @@
 
 
 def reduce_kernel(
-    hid,
-    up,
+    hid_hbm,
+    up_hbm,
     counts,
-    cot,
-    rin,
+    cot_hbm,
+    rin_hbm,
     grad,
     rgrad,
     total,
+    hid,
+    up,
+    cot,
+    rin,
     hid_t,
     terms,
     x_out,
@@ -90,7 +94,10 @@
     r_in2,
     r3,
     r_in3,
-    sums,
+    piece,
+    plane_sums,
+    side_sums,
+    load_sem,
     x_ssem,
     x_rsem,
     z_ssem,
@@ -125,15 +132,28 @@
         return {"e": e + 1 - 2 * core}
 
     pair = {"zl": 1 - zl}
-    axes = ((at_x, 4, x), (at_z, 4, z), (at_y, 4, y), (at_core, 2, core))
-
+
+    def at_plane(j):
+        there = (z + j % 4) % 4
+        return {"x": (x + j // 4) % 4, "zl": there % 2, "e": y * 4 + (there // 2) * 2 + core}
+
+    def at_side(j):
+        return {"e": ((y + j // 2) % 4) * 4 + zh * 2 + (core + j) % 2}
+
+    loads = [
+        pltpu.make_async_copy(src, dst, load_sem.at[n])
+        for n, (src, dst) in enumerate(((hid_hbm, hid), (up_hbm, up), (cot_hbm, cot), (rin_hbm, rin)))
+    ]
+    for copy in loads:
+        copy.start()
     barrier = pltpu.get_barrier_semaphore()
-    for at, size, _ in axes:
+    for at, size in ((at_plane, 16), (at_side, 8)):
         for j in range(1, size):
             pl.semaphore_signal(barrier, inc=1, device_id=at(j), device_id_type=MESH)
 
     live = counts[0, 0]
     keep = (lax.broadcasted_iota(jnp.int32, (depth, LANES), 0) < live).astype(F32).astype(jnp.bfloat16)
+    loads[0].wait()
 
     @pl.loop(0, units // LANES)
     def _(t):
@@ -205,8 +225,9 @@
     far, right, left = (x + 2) % 4, (x + 1) % 4, (x + 3) % 4
     a_at, b_at = early, early + late_a
 
+    loads[1].wait()
     multiply(far)
-    pl.semaphore_wait(barrier, 10)
+    pl.semaphore_wait(barrier, 22)
     e0 = early_part(far, 0, 3)
     multiply(4 + far)
     e1 = early_part(4 + far, 1, 1)
@@ -218,6 +239,8 @@
     multiply(4 + right)
     p1 = pair_part(1, right)
 
+    loads[2].wait()
+    loads[3].wait()
     rp[...] = jnp.dot(cot[...], rin[...], preferred_element_type=F32)
     n_router = rp.shape[0]
     r_half, r_cols = n_router // 2, wide // 4
@@ -271,28 +294,6 @@
     p1.wait_recv()
     pair_sum(1, right)
     l2 = late_part(right, a_at, late_a, 2, 1)
-    p2.wait_recv()
-    pair_sum(2, left)
-    l3 = late_part(left, b_at, late_b, 3, 3)
-
-    for copy in (e2, e3, e4, e5):
-        copy.wait_recv()
-
-    def fold(r, i):
-        terms[x, r, :] += decode_rows(x_in.at[2], i, wide) + decode_rows(x_in.at[4], i, wide)
-        terms[4 + x, r, :] += decode_rows(x_in.at[3], i, wide) + decode_rows(x_in.at[5], i, wide)
-        encode_rows(terms[(1 - zl) * 4 + x, r, :], last_out, i)
-
-    tiles(0, early, fold)
-    last = send(last_out, last_in, z_ssem.at[4], z_rsem.at[4], pair)
-
-    l0.wait_recv()
-    l4 = late_part(left, a_at, late_a, 4, 3, 0)
-    l1.wait_recv()
-    l5 = late_part(right, b_at, late_b, 5, 1, 1)
-    p3.wait_recv()
-    pair_sum(3, x)
-
     for copy in s2:
         copy.wait_recv()
     r3[...] = r2[:, pl.ds(pl.multiple_of(z * r_cols, LANES), r_cols)] + r_in2[0] + r_in2[1] + r_in2[2]
@@ -306,6 +307,46 @@
         )
         for j in range(1, 4)
     ]
+    p2.wait_recv()
+    pair_sum(2, left)
+    l3 = late_part(left, b_at, late_b, 3, 3)
+
+    for copy in (e2, e3, e4, e5):
+        copy.wait_recv()
+
+    def fold(r, i):
+        terms[x, r, :] += decode_rows(x_in.at[2], i, wide) + decode_rows(x_in.at[4], i, wide)
+        terms[4 + x, r, :] += decode_rows(x_in.at[3], i, wide) + decode_rows(x_in.at[5], i, wide)
+        encode_rows(terms[(1 - zl) * 4 + x, r, :], last_out, i)
+
+    tiles(0, early, fold)
+    last = send(last_out, last_in, z_ssem.at[4], z_rsem.at[4], pair)
+    for copy in s3:
+        copy.wait_recv()
+    piece[...] = r3[:, pl.ds(pl.multiple_of(x * LANES, LANES), LANES)] + r_in3[0] + r_in3[1] + r_in3[2]
+    my_row = core * r_half + y * 8
+    z_col = z * r_cols
+    x_col = z_col + x * LANES
+    rgrad[pl.ds(pl.multiple_of(my_row, 8), 8), pl.ds(pl.multiple_of(x_col, LANES), LANES)] = piece[...]
+
+    def give_back(stage, row, height, col, width, at, size):
+        part = rgrad.at[pl.ds(pl.multiple_of(row, 8), height), pl.ds(pl.multiple_of(col, LANES), width)]
+        return [
+            send(part, part, r_ssem.at[stage, j], r_rsem.at[stage, j], at(j)) for j in range(1, size)
+        ]
+
+    b0 = give_back(4, my_row, 8, x_col, LANES, at_x, 4)
+
+
+    l0.wait_recv()
+    l4 = late_part(left, a_at, late_a, 4, 3, 0)
+    l1.wait_recv()
+    l5 = late_part(right, b_at, late_b, 5, 1, 1)
+    p3.wait_recv()
+    pair_sum(3, x)
+    for copy in b0:
+        copy.wait_recv()
+    b1 = give_back(5, my_row, 8, z_col, r_cols, at_z, 4)
 
     own = zl * 4 + x
 
@@ -331,6 +372,9 @@
     squares = jnp.zeros((8, LANES), F32)
     last.wait_recv()
     squares = close(0, early, squares, (last_in,))
+    for copy in b1:
+        copy.wait_recv()
+    b2 = give_back(6, my_row, 8, 0, wide, at_y, 4)
     for copy in (l2, l4):
         copy.wait_recv()
     squares = close(a_at, late_a, squares, (late_in.at[2], late_in.at[4]))
@@ -338,46 +382,33 @@
         copy.wait_recv()
     squares = close(b_at, late_b, squares, (late_in.at[3], late_in.at[5]))
 
-    for copy in s3:
-        copy.wait_recv()
-    piece = r3[:, pl.ds(pl.multiple_of(x * LANES, LANES), LANES)] + r_in3[0] + r_in3[1] + r_in3[2]
-    squares = squares + piece * piece
-    my_row = core * r_half + y * 8
-    z_col = z * r_cols
-    x_col = z_col + x * LANES
-    rgrad[pl.ds(pl.multiple_of(my_row, 8), 8), pl.ds(pl.multiple_of(x_col, LANES), LANES)] = piece
-
-    waits = [e0, e1, e2, e3, e4, e5, l0, l1, l2, l3, l4, l5, p0, p1, p2, p3, last, s0, *s1, *s2, *s3]
-    spread = (
-        (my_row, 8, x_col, LANES),
-        (my_row, 8, z_col, r_cols),
-        (my_row, 8, 0, wide),
-        (core * r_half, r_half, 0, wide),
-    )
-    back = []
-    for stage, (at, size, here) in enumerate(axes):
-        sums[stage, here] = squares
-        mine = sums.at[stage, here]
-        group = [
-            send(mine, mine, n_ssem.at[stage, j], n_rsem.at[stage, j], at(j)) for j in range(1, size)
-        ]
-        for copy in back:
-            copy.wait_recv()
-        row, height, col, width = spread[stage]
-        part = rgrad.at[pl.ds(pl.multiple_of(row, 8), height), pl.ds(pl.multiple_of(col, LANES), width)]
-        back = [
-            send(part, part, r_ssem.at[4 + stage, j], r_rsem.at[4 + stage, j], at(j)) for j in range(1, size)
-        ]
-        waits += group + back
+    squares = squares + piece[...] * piece[...]
+
+    def tell(buf, here, at, size, sem):
+        buf[here] = squares
+        mine = buf.at[here]
+        return [send(mine, mine, n_ssem.at[sem + j], n_rsem.at[sem + j], at(j)) for j in range(1, size)]
+
+    def sum_of(buf, size, group):
         for copy in group:
             copy.wait_recv()
-        squares = sums[stage, 0]
+        acc = buf[0]
         for k in range(1, size):
-            squares = squares + sums[stage, k]
+            acc = acc + buf[k]
+        return acc
+
+    plane_copies = tell(plane_sums, x * 4 + z, at_plane, 16, 0)
+    for copy in b2:
+        copy.wait_recv()
+    b3 = give_back(7, core * r_half, r_half, 0, wide, at_core, 2)
+    squares = sum_of(plane_sums, 16, plane_copies)
+    side_copies = tell(side_sums, y * 2 + core, at_side, 8, 16)
+    squares = sum_of(side_sums, 8, side_copies)
     total[...] = jnp.broadcast_to(jnp.sum(squares), total.shape)
-    for copy in back:
-        copy.wait_recv()
-    for copy in waits:
+    for copy in b3:
+        copy.wait_recv()
+    waits = [e0, e1, e2, e3, e4, e5, l0, l1, l2, l3, l4, l5, p0, p1, p2, p3, last, s0, *s1, *s2, *s3]
+    for copy in waits + b0 + b1 + b2 + b3 + plane_copies + side_copies:
         copy.wait_send()
 
 
@@ -387,6 +418,10 @@
     ratio = first_new / correct_first / (jnp.sqrt(second_new / correct_second) + adam_eps)
     weights_new = weights - learn_rate * (ratio + decay_weight * weights)
     return (weights_new, first_new, second_new)
+
+
+def in_hbm(array):
+    return pltpu.with_memory_space_constraint(array, pltpu.HBM)
 
 
 def each(act, start=1):
@@ -409,12 +444,23 @@
     new_master,
     new_first,
     new_second,
+    lead_out0,
+    lead_out1,
+    lead_mid0,
+    lead_mid1,
+    lead_turn0,
+    lead_turn1,
+    lead_land0,
+    lead_land1,
+    lead_twin0,
+    lead_twin1,
     leaving,
     middle0,
     middle1,
-    middle2,
     turned,
     landed,
+    l_ssem,
+    l_rsem,
     ssem,
     rsem,
     a_ssem,
@@ -423,20 +469,26 @@
     zl, x, e = (lax.axis_index(a) for a in ALL)
     rows, wide = grad.shape
     half = wide // 2
-    results = (new_master, new_first, new_second)
-    middle = (middle0, middle1, middle2)
+    results = (new_first, new_second)
+    lead_out, lead_mid = (lead_out0, lead_out1), (lead_mid0, lead_mid1)
+    lead_turn, lead_land, lead_twin = (lead_turn0, lead_turn1), (lead_land0, lead_land1), (lead_twin0, lead_twin1)
+    middle = (middle0, middle1)
+    split = lead_out0.shape[1] - 16
+    runs = ((0, split), (split, rows - split))
 
     def peer(j):
         return {"e": (e + j) % GROUPS}
 
+    def twin_peer(j):
+        return {"e": (e + j) % GROUPS, "zl": 1 - zl}
+
     def at_x(j):
         return {"x": (x + j) % 4}
 
-    pair = {"zl": 1 - zl}
-
     barrier = pltpu.get_barrier_semaphore()
     each(lambda j: pl.semaphore_signal(barrier, inc=1, device_id=peer(j), device_id_type=MESH))
-    for device in (at_x(1), at_x(3), pair):
+    each(lambda j: pl.semaphore_signal(barrier, inc=1, device_id=twin_peer(j), device_id_type=MESH), 0)
+    for device in (at_x(1), at_x(3)):
         pl.semaphore_signal(barrier, inc=1, device_id=device, device_id_type=MESH)
 
     factor = jnp.minimum(1.0, limit / (jnp.sqrt(total[0:1, 0:1]) + norm_eps))
@@ -444,129 +496,172 @@
     def columns(g):
         return pl.ds(pl.multiple_of(g * LANES, LANES), LANES)
 
-    def update(g):
-        c = columns(g)
-        return adam_update(factor * grad[:, c], first[:, c], second[:, c], master[:, c])
-
-    def encode(k, g, values):
+    def update(g, start=0, size=rows):
+        c, r = columns(g), pl.ds(start, size)
+        return adam_update(factor * grad[r, c], first[r, c], second[r, c], master[r, c])
+
+    def pack(piece, size, values):
         code = code_of(jnp.max(jnp.abs(values), axis=0, keepdims=True))
-        leaving[k, g, 0:rows, :] = to_codes(values, code)
-        leaving[k, g, rows:, :] = jnp.broadcast_to(code, (16, LANES)).astype(I16)
-
-    def decode(k, g):
-        piece = landed.at[k, g]
-        values = piece[0:rows, :].astype(F32) * scale_of(piece[rows : rows + 1, :].astype(F32))
-        results[k][:, columns(g)] = values
-        return values
-
-    def remote(src, dst, phase, k, j):
+        piece[0:size, :] = to_codes(values, code)
+        piece[size:, :] = jnp.broadcast_to(code, (16, LANES)).astype(I16)
+
+    def unpack(piece, size):
+        return piece[0:size, :].astype(F32) * scale_of(piece[size : size + 1, :].astype(F32))
+
+    def remote(src, dst, send_sem, recv_sem, device):
         return pltpu.make_async_remote_copy(
             src_ref=src,
             dst_ref=dst,
-            send_sem=ssem.at[phase, k, j],
-            recv_sem=rsem.at[phase, k, j],
-            device_id=peer(j),
+            send_sem=send_sem,
+            recv_sem=recv_sem,
+            device_id=device,
             device_id_type=MESH,
         )
 
+    def lead_go(h, j):
+        at = (0, h, j)
+        return remote(lead_out[h].at[(e + j) % GROUPS], lead_mid[h].at[j], l_ssem.at[at], l_rsem.at[at], peer(j))
+
+    def lead_come(h, j):
+        at = (1, h, j)
+        src = lead_turn[h].at[(e + j) % GROUPS]
+        return remote(src, lead_land[h].at[e], l_ssem.at[at], l_rsem.at[at], peer(j))
+
+    def lead_cross(h, j):
+        at = (2, h, j)
+        src = lead_turn[h].at[(e + j) % GROUPS]
+        return remote(src, lead_twin[h].at[e], l_ssem.at[at], l_rsem.at[at], twin_peer(j))
+
     def go(k, j):
-        return remote(leaving.at[k, (e + j) % GROUPS], middle[k].at[j], 0, k, j)
+        at = (0, k, j)
+        return remote(leaving.at[k, (e + j) % GROUPS], middle[k].at[j], ssem.at[at], rsem.at[at], peer(j))
 
     def come(k, j):
-        return remote(turned.at[k, (e + j) % GROUPS], landed.at[k, e], 1, k, j)
-
-    def permute(k):
-        middle[k][0] = leaving[k, e]
-
+        at = (1, k, j)
+        return remote(turned.at[k, (e + j) % GROUPS], landed.at[k, e], ssem.at[at], rsem.at[at], peer(j))
+
+    def permute(arrived, to):
         def step(p, carry):
-            turned[k, p] = middle[k][(e - partner[p] + GROUPS) % GROUPS]
+            to[p] = arrived[(e - partner[p] + GROUPS) % GROUPS]
             return carry
 
         lax.fori_loop(0, GROUPS, step, 0)
+
+    for h, run in enumerate(runs):
+        pack(lead_out[h].at[e], run[1], update(e, *run)[0])
+    pl.semaphore_wait(barrier, 2 * GROUPS + 1)
+    for h, run in enumerate(runs):
+
+        def first_leg(j, h=h, run=run):
+            g = (e + j) % GROUPS
+            pack(lead_out[h].at[g], run[1], update(g, *run)[0])
+            lead_go(h, j).start()
+
+        each(first_leg)
+        lead_mid[h][0] = lead_out[h][e]
+
+    for h in range(2):
+        each(lambda j, h=h: lead_go(h, j).wait_recv())
+        permute(lead_mid[h], lead_turn[h])
+        each(lambda j, h=h: lead_come(h, j).start())
+        lead_land[h][e] = lead_turn[h][e]
+    for h in range(2):
+        each(lambda j, h=h: lead_cross(h, j).start(), 0)
+
+    def moments(g):
+        _, first_new, second_new = update(g)
+        pack(leaving.at[0, g], rows, first_new)
+        pack(leaving.at[1, g], rows, second_new)
+
+    each(moments, 0)
+
+    own, twin = zl * 4 + x, (1 - zl) * 4 + x
+    left, right = (x + 3) % 4, (x + 1) % 4
+
+    def weight_rows(block, h):
+        return pl.ds(pl.multiple_of(block * rows + runs[h][0], 16), runs[h][1])
+
+    def gather(n, h, block, col, width, device):
+        part = weight.at[weight_rows(block, h), pl.ds(col, width)]
+        return send(part, part, a_ssem.at[n, h], a_rsem.at[n, h], device)
+
+    def settle(h, g):
+        values = unpack(lead_land[h].at[g], runs[h][1])
+        new_master[pl.ds(*runs[h]), columns(g)] = values
+        weight[weight_rows(own, h), columns(g)] = values.astype(jnp.bfloat16)
+
+    def settle_twin(h, g):
+        values = unpack(lead_twin[h].at[g], runs[h][1])
+        weight[weight_rows(twin, h), columns(g)] = values.astype(jnp.bfloat16)
+
+    to_right, to_left = [], []
+    for h in range(2):
+        settle(h, e)
+
+        def settle_next(j, h=h):
+            lead_come(h, j).wait_recv()
+            settle(h, (e - j + GROUPS) % GROUPS)
+
+        each(settle_next)
+        to_right.append(gather(0, h, own, 0, wide, at_x(1)))
+        to_left.append(gather(1, h, own, 0, wide, at_x(3)))
+
+    each(lambda j: go(0, j).start())
+    each(lambda j: go(1, j).start())
+
+    twin_right, twin_left = [], []
+    for h in range(2):
+
+        def settle_cross(j, h=h):
+            lead_cross(h, j).wait_recv()
+            settle_twin(h, (e - j + GROUPS) % GROUPS)
+
+        each(settle_cross, 0)
+        twin_right.append(gather(2, h, twin, 0, wide, at_x(1)))
+        twin_left.append(gather(3, h, twin, 0, wide, at_x(3)))
+
+    onward = []
+
+    def pass_on(n, h, z_at, from_left, from_right):
+        from_left.wait_recv()
+        onward.append(gather(n, h, z_at * 4 + left, 0, half, at_x(1)))
+        from_right.wait_recv()
+        onward.append(gather(n + 1, h, z_at * 4 + right, half, half, at_x(3)))
 
     def turn(k):
         each(lambda j: go(k, j).wait_recv())
-        permute(k)
+        middle[k][0] = leaving[k, e]
+        permute(middle[k], turned.at[k])
         each(lambda j: come(k, j).start())
         landed[k, e] = turned[k, e]
 
-    encode(0, e, update(e)[0])
-    pl.semaphore_wait(barrier, GROUPS + 2)
-
-    def first_leg(j):
-        g = (e + j) % GROUPS
-        encode(0, g, update(g)[0])
-        go(0, j).start()
-
-    each(first_leg)
-
-    def moments(g):
-        _, first_new, second_new = update(g)
-        encode(1, g, first_new)
-        encode(2, g, second_new)
-
-    each(moments, 0)
+    pass_on(4, 0, zl, to_right[0], to_left[0])
+    pass_on(4, 1, zl, to_right[1], to_left[1])
     turn(0)
-
-    def weight_part(block, col, width):
-        return weight.at[
-            pl.ds(pl.multiple_of(block * rows, 16), rows), pl.ds(pl.multiple_of(col, LANES), width)
-        ]
-
-    own, twin = zl * 4 + x, (1 - zl) * 4 + x
-    own_rows = pl.ds(pl.multiple_of(own * rows, 16), rows)
-
-    def settle(g):
-        weight[own_rows, columns(g)] = decode(0, g).astype(jnp.bfloat16)
-
-    settle(e)
-
-    def settle_next(j):
-        come(0, j).wait_recv()
-        settle((e - j + GROUPS) % GROUPS)
-
-    each(settle_next)
-
-    def gather(n, block, col, width, device):
-        part = weight_part(block, col, width)
-        return send(part, part, a_ssem.at[n], a_rsem.at[n], device)
-
-    left, right = (x + 3) % 4, (x + 1) % 4
-    g_pair = gather(0, own, 0, wide, pair)
-    g_right = gather(1, own, 0, wide, at_x(1))
-    g_left = gather(2, own, 0, wide, at_x(3))
-    each(lambda j: go(1, j).start())
-    each(lambda j: go(2, j).start())
-
-    g_pair.wait_recv()
-    t_right = gather(3, twin, 0, wide, at_x(1))
-    t_left = gather(4, twin, 0, wide, at_x(3))
-    g_right.wait_recv()
-    f_right = gather(5, zl * 4 + left, 0, half, at_x(1))
-    g_left.wait_recv()
-    f_left = gather(6, zl * 4 + right, half, half, at_x(3))
-
+    pass_on(6, 0, 1 - zl, twin_right[0], twin_left[0])
     turn(1)
-    t_right.wait_recv()
-    h_right = gather(7, (1 - zl) * 4 + left, 0, half, at_x(1))
-    t_left.wait_recv()
-    h_left = gather(8, (1 - zl) * 4 + right, half, half, at_x(3))
-    turn(2)
-
-    for k in (1, 2):
-        decode(k, e)
-
-        def finish(j, k=k):
+    pass_on(6, 1, 1 - zl, twin_right[1], twin_left[1])
+
+    for k in range(2):
+
+        def finish(g, k=k):
+            results[k][:, columns(g)] = unpack(landed.at[k, g], rows)
+
+        def finish_next(j, k=k, finish=finish):
             come(k, j).wait_recv()
-            decode(k, (e - j + GROUPS) % GROUPS)
-
-        each(finish)
-    for copy in (f_right, f_left, h_right, h_left):
-        copy.wait_recv()
-    for k in range(3):
+            finish((e - j + GROUPS) % GROUPS)
+
+        finish(e)
+        each(finish_next)
+    for copy in onward:
+        copy.wait_recv()
+    for k in range(2):
+        each(lambda j, k=k: lead_go(k, j).wait_send())
+        each(lambda j, k=k: lead_come(k, j).wait_send())
+        each(lambda j, k=k: lead_cross(k, j).wait_send(), 0)
         each(lambda j, k=k: go(k, j).wait_send())
         each(lambda j, k=k: come(k, j).wait_send())
-    for copy in (g_pair, g_right, g_left, t_right, t_left, f_right, f_left, h_right, h_left):
+    for copy in to_right + to_left + twin_right + twin_left + onward:
         copy.wait_send()
 
 
@@ -590,6 +685,7 @@
     n_router = router_cot.shape[0]
     vmem = pl.BlockSpec(memory_space=pltpu.VMEM)
     smem = pl.BlockSpec(memory_space=pltpu.SMEM)
+    hbm = pl.BlockSpec(memory_space=pltpu.HBM)
     dma = pltpu.SemaphoreType.DMA
     coded = wide + LANES
     r_half, r_cols = n_router // 2, wide // 4
@@ -603,9 +699,13 @@
             jax.ShapeDtypeStruct((n_router, wide), F32),
             jax.ShapeDtypeStruct((8, LANES), F32),
         ),
-        in_specs=[vmem, vmem, smem, vmem, vmem],
+        in_specs=[hbm, hbm, smem, hbm, hbm],
         out_specs=(vmem, vmem, vmem),
         scratch_shapes=[
+            pltpu.VMEM((depth, units), jnp.bfloat16),
+            pltpu.VMEM((depth, wide), jnp.bfloat16),
+            pltpu.VMEM(router_cot.shape, jnp.bfloat16),
+            pltpu.VMEM(router_input.shape, jnp.bfloat16),
             pltpu.VMEM((units, depth), jnp.bfloat16),
             pltpu.VMEM((8, rows, wide), F32),
             *[pltpu.VMEM((6, early, coded), I16)] * 2,
@@ -620,24 +720,28 @@
             pltpu.VMEM((3, 8, r_cols), F32),
             pltpu.VMEM((8, r_cols), F32),
             pltpu.VMEM((3, 8, LANES), F32),
-            pltpu.VMEM((4, 4, 8, LANES), F32),
+            pltpu.VMEM((8, LANES), F32),
+            pltpu.VMEM((16, 8, LANES), F32),
+            pltpu.VMEM((8, 8, LANES), F32),
+            dma((4,)),
             dma((12,)),
             dma((12,)),
             dma((5,)),
             dma((5,)),
             dma((8, 4)),
             dma((8, 4)),
-            dma((4, 4)),
-            dma((4, 4)),
+            dma((24,)),
+            dma((24,)),
         ],
         compiler_params=pltpu.CompilerParams(
             collective_id=0, has_side_effects=True, vmem_limit_bytes=40 * 1024 * 1024
         ),
         name="reduce",
-    )(hidden[0], upstream[0], token_counts, router_cot, router_input)
+    )(in_hbm(hidden[0]), in_hbm(upstream[0]), token_counts, in_hbm(router_cot), in_hbm(router_input))
 
     clip_limit = 2.0 * math.sqrt(float(GROUPS * units * wide + n_router * wide))
     tall = rows + 16
+    split = (rows // 16 + 1) // 2 * 16
     state = jax.ShapeDtypeStruct((rows, wide), F32)
     weight, new_master, new_first, new_second = pl.pallas_call(
         functools.partial(move_kernel, clip_limit),
@@ -645,13 +749,16 @@
         in_specs=[vmem, vmem, vmem, vmem, vmem, smem],
         out_specs=(vmem, vmem, vmem, vmem),
         scratch_shapes=[
-            pltpu.VMEM((3, GROUPS, tall, LANES), I16),
-            *[pltpu.VMEM((GROUPS, tall, LANES), I16)] * 3,
-            *[pltpu.VMEM((3, GROUPS, tall, LANES), I16)] * 2,
-            dma((2, 3, GROUPS)),
-            dma((2, 3, GROUPS)),
-            dma((9,)),
-            dma((9,)),
+            *[pltpu.VMEM((GROUPS, n, LANES), I16) for n in (split + 16, rows - split + 16)] * 5,
+            pltpu.VMEM((2, GROUPS, tall, LANES), I16),
+            *[pltpu.VMEM((GROUPS, tall, LANES), I16)] * 2,
+            *[pltpu.VMEM((2, GROUPS, tall, LANES), I16)] * 2,
+            dma((3, 2, GROUPS)),
+            dma((3, 2, GROUPS)),
+            dma((2, 2, GROUPS)),
+            dma((2, 2, GROUPS)),
+            dma((8, 2)),
+            dma((8, 2)),
         ],
         compiler_params=pltpu.CompilerParams(
             collective_id=1, has_side_effects=True, vmem_limit_bytes=27 * 1024 * 1024

time: 177 us -> 155 us (0.88)
  Pallas kernels: 161 us -> 144 us
  local copies, waits for them, and re-layouts: 12.4 us -> 6.38 us
    pallas_call x1, Pallas kernels: 92 us -> 75.4 us  [on_device(): pl.pallas_call(functools.partial(move_kernel, clip_limit), out_shape=(jax...]
    unnamed x26 -> x18, local copies, waits for them, and re-layouts: 11.9 us -> 5.86 us
where the time goes in v3:
time: 155 us; the launch traced here: 154 us
  Pallas kernels  144 us (93%)
  local copies, waits for them, and re-layouts  6.38 us (4%)
  between operations  2.14 us (1%)
    pallas_call x1, Pallas kernels, on_device(): pl.pallas_call(functools.partial(move_kernel, clip_limit), out_shape=(jax...  75.4 us
    pallas_call x1, Pallas kernels, on_device(): pl.pallas_call(reduce_kernel, out_shape=(jax.ShapeDtypeStruct((rows, wide...  69.1 us
    unnamed x18, local copies, waits for them, and re-layouts  5.86 us

profile of v3, /device:TPU:1, one launch (start us, length us, event | category | flops | bytes accessed | tf_op | source)
XLA Modules:
  0.0 154.4 jit_solution(18130792936418747199)
XLA Ops:
  1.3 0.0 copy-start
  1.3 0.0 copy-start.1
  1.3 0.0 copy-start.2
  1.3 0.0 copy-start.3
  1.3 69.1 %reduce.1 = (f32[176,2048]{1,0:T(8,128)S(1)}, f32[64,2048]{1,0:T(8,128)S(1)}, f32[8,128]{1,0:T(8,128)S(1)}) custom-call(bf16[1152,1408]{1,0:T(8,128)(2,1)} %bitcast.18, bf16[1152,2048]{1,0:T(8,128)(2,1)} %bitcast.17, s32[1,1]{1,0:T(1,128)S(6)} %copy.23.counts, bf16[64,128]{1,0:T(8,128)(2,1)} %cot_hbm.1, bf16[128,2048]{1,0:T(8,128)(2,1)} %rin_hbm.1), custom_call_target="tpu_custom_call" | custom-call | tf_op jit(solution)/shard_map/reduce/pallas_call | solution.py:695
  70.4 0.0 copy-done
  70.4 0.0 copy-done.1
  70.4 0.0 copy-done.2
  70.4 0.0 copy-done.3
  70.4 0.0 copy-start.4
  70.4 0.0 copy-start.5
  70.5 0.0 copy-start.6
  70.5 75.4 %move.1 = (bf16[1408,2048]{1,0:T(8,128)(2,1)S(1)}, f32[176,2048]{1,0:T(8,128)S(1)}, f32[176,2048]{1,0:T(8,128)S(1)}, f32[176,2048]{1,0:T(8,128)S(1)}) custom-call(f32[176,2048]{1,0:T(8,128)S(1)} %get-tuple-element.14.grad, f32[8,128]{1,0:T(8,128)S(1)} %get-tuple-element.15.total, f32[176,2048]{1,0:T(8,128)S(1)} %bitcast.14, f32[176,2048]{1,0:T(8,128)S(1)} %bitcast.15, ...), custom_call_target="tpu_custom_call" | custom-call | tf_op jit(solution)/shard_map/move/pallas_call | solution.py:746
  145.9 0.5 slice.3
  147.2 0.0 copy-done.4
  147.2 0.0 copy-done.5
  147.2 0.0 copy-done.6
  147.2 1.4 multiply_subtract_fusion
  148.6 2.5 %copy.24 = bf16[1,1408,2048]{2,1,0:T(8,128)(2,1)} copy(bf16[1,1408,2048]{2,1,0:T(8,128)(2,1)S(1)} %bitcast.10) | data formatting | bytes 11534336
  151.1 1.1 copy.25
  152.2 1.1 copy.26
  153.3 1.1 copy.27
Async XLA Ops:
  1.3 69.1 %copy-start = (f32[1,176,2048]{2,1,0:T(8,128)S(1)}, f32[1,176,2048]{2,1,0:T(8,128)}, u32[]{:S(2)}) copy-start(f32[1,176,2048]{2,1,0:T(8,128)} %param.15) | copy-start | bytes 4325380
  1.3 69.1 %copy-start.1 = (f32[1,176,2048]{2,1,0:T(8,128)S(1)}, f32[1,176,2048]{2,1,0:T(8,128)}, u32[]{:S(2)}) copy-start(f32[1,176,2048]{2,1,0:T(8,128)} %param.16) | copy-start | bytes 4325380
  1.3 69.1 %copy-start.2 = (f32[1,176,2048]{2,1,0:T(8,128)S(1)}, f32[1,176,2048]{2,1,0:T(8,128)}, u32[]{:S(2)}) copy-start(f32[1,176,2048]{2,1,0:T(8,128)} %param.17) | copy-start | bytes 4325380
  1.3 69.1 %copy-start.3 = (s32[16]{0:T(128)S(1)}, s32[16]{0:T(128)}, u32[]{:S(2)}) copy-start(s32[16]{0:T(128)} %partner.1) | copy-start | bytes 196
  70.4 76.7 %copy-start.4 = (f32[64,2048]{1,0:T(8,128)S(1)}, f32[64,2048]{1,0:T(8,128)}, u32[]{:S(2)}) copy-start(f32[64,2048]{1,0:T(8,128)} %param.20) | copy-start | bytes 1572868
  70.4 76.7 %copy-start.5 = (f32[64,2048]{1,0:T(8,128)S(1)}, f32[64,2048]{1,0:T(8,128)}, u32[]{:S(2)}) copy-start(f32[64,2048]{1,0:T(8,128)} %param.21) | copy-start | bytes 1572868
  70.5 76.7 %copy-start.6 = (f32[64,2048]{1,0:T(8,128)S(1)}, f32[64,2048]{1,0:T(8,128)}, u32[]{:S(2)}) copy-start(f32[64,2048]{1,0:T(8,128)} %param.22) | copy-start | bytes 1572868

commit v4 on v3

--- a/solution.py
+++ b/solution.py
@@ -176,8 +176,20 @@
                 pl.ds(pl.multiple_of(i * 16, 16), 16),
             )
 
+    def x_made(slot, device):
+        return pltpu.make_async_remote_copy(
+            src_ref=x_out.at[slot],
+            dst_ref=x_in.at[slot],
+            send_sem=x_ssem.at[slot],
+            recv_sem=x_rsem.at[slot],
+            device_id=device,
+            device_id_type=MESH,
+        )
+
     def x_copy(slot, device):
-        return send(x_out.at[slot], x_in.at[slot], x_ssem.at[slot], x_rsem.at[slot], device)
+        copy = x_made(slot, device)
+        copy.start()
+        return copy
 
     def late_copy(slot, size, device):
         r = pl.ds(0, size)
@@ -226,12 +238,13 @@
     a_at, b_at = early, early + late_a
 
     loads[1].wait()
-    multiply(far)
+    multiply((1 - zl) * 4 + far)
     pl.semaphore_wait(barrier, 22)
-    e0 = early_part(far, 0, 3)
-    multiply(4 + far)
-    e1 = early_part(4 + far, 1, 1)
     p0 = pair_part(0, far)
+    early_part((1 - zl) * 4 + far, 1 - zl, 1 + 2 * zl)
+    multiply(zl * 4 + far)
+    early_part(zl * 4 + far, zl, 3 - 2 * zl)
+    e0, e1 = x_made(0, at_x(3)), x_made(1, at_x(1))
     multiply(right)
     e2 = early_part(right, 2, 1)
     multiply(4 + left)
@@ -432,6 +445,56 @@
     lax.fori_loop(start, GROUPS, step, 0)
 
 
+def unpack(piece, size, codes):
+    return piece[0:size, :].astype(F32) * scale_of(codes.astype(F32))
+
+
+def close_kernel(
+    limit,
+    weight,
+    new_master,
+    landed0,
+    landed1,
+    total,
+    rgrad,
+    r_master,
+    r_first,
+    r_second,
+    weight_out,
+    master_out,
+    first_out,
+    second_out,
+    r_master_out,
+    r_first_out,
+    r_second_out,
+    values,
+    r_values,
+    sem,
+):
+    rows = new_master.shape[0]
+    copies = []
+
+    def put(src, dst):
+        copy = pltpu.make_async_copy(src, dst, sem.at[len(copies)])
+        copy.start()
+        copies.append(copy)
+
+    put(weight, weight_out)
+    put(new_master, master_out)
+    for k, (landed, out) in enumerate(((landed0, first_out), (landed1, second_out))):
+        for g in range(GROUPS):
+            code = landed0[g, rows + 8 * k : rows + 8 * k + 1, :]
+            values[k, :, g * LANES : (g + 1) * LANES] = unpack(landed.at[g], rows, code)
+        put(values.at[k], out)
+    factor = jnp.minimum(1.0, limit / (jnp.sqrt(total[0:1, 0:1]) + norm_eps))
+    new = adam_update(factor * rgrad[...], r_first[...], r_second[...], r_master[...])
+    for k, out in enumerate((r_master_out, r_first_out, r_second_out)):
+        r_values[k] = new[k]
+        put(r_values.at[k], out)
+    for copy in copies:
+        copy.wait()
+
+
 def move_kernel(
     limit,
     grad,
@@ -442,8 +505,8 @@
     partner,
     weight,
     new_master,
-    new_first,
-    new_second,
+    landed0,
+    landed1,
     lead_out0,
     lead_out1,
     lead_mid0,
@@ -454,11 +517,12 @@
     lead_land1,
     lead_twin0,
     lead_twin1,
-    leaving,
+    leaving0,
+    leaving1,
     middle0,
     middle1,
-    turned,
-    landed,
+    turned0,
+    turned1,
     l_ssem,
     l_rsem,
     ssem,
@@ -469,10 +533,10 @@
     zl, x, e = (lax.axis_index(a) for a in ALL)
     rows, wide = grad.shape
     half = wide // 2
-    results = (new_first, new_second)
     lead_out, lead_mid = (lead_out0, lead_out1), (lead_mid0, lead_mid1)
     lead_turn, lead_land, lead_twin = (lead_turn0, lead_turn1), (lead_land0, lead_land1), (lead_twin0, lead_twin1)
-    middle = (middle0, middle1)
+    leaving, middle = (leaving0, leaving1), (middle0, middle1)
+    turned, landed = (turned0, turned1), (landed0, landed1)
     split = lead_out0.shape[1] - 16
     runs = ((0, split), (split, rows - split))
 
@@ -496,17 +560,19 @@
     def columns(g):
         return pl.ds(pl.multiple_of(g * LANES, LANES), LANES)
 
-    def update(g, start=0, size=rows):
-        c, r = columns(g), pl.ds(start, size)
-        return adam_update(factor * grad[r, c], first[r, c], second[r, c], master[r, c])
-
-    def pack(piece, size, values):
-        code = code_of(jnp.max(jnp.abs(values), axis=0, keepdims=True))
-        piece[0:size, :] = to_codes(values, code)
-        piece[size:, :] = jnp.broadcast_to(code, (16, LANES)).astype(I16)
-
-    def unpack(piece, size):
-        return piece[0:size, :].astype(F32) * scale_of(piece[size : size + 1, :].astype(F32))
+    def update(g):
+        c = columns(g)
+        return adam_update(factor * grad[:, c], first[:, c], second[:, c], master[:, c])
+
+    def column_code(values):
+        return code_of(jnp.max(jnp.abs(values), axis=0, keepdims=True))
+
+    def pack_lead(g):
+        values = update(g)[0]
+        code = column_code(values)
+        for h, (start, size) in enumerate(runs):
+            lead_out[h][g, 0:size, :] = to_codes(values[start : start + size], code)
+        lead_out[0][g, split:, :] = jnp.broadcast_to(code, (16, LANES)).astype(I16)
 
     def remote(src, dst, send_sem, recv_sem, device):
         return pltpu.make_async_remote_copy(
@@ -534,11 +600,11 @@
 
     def go(k, j):
         at = (0, k, j)
-        return remote(leaving.at[k, (e + j) % GROUPS], middle[k].at[j], ssem.at[at], rsem.at[at], peer(j))
+        return remote(leaving[k].at[(e + j) % GROUPS], middle[k].at[j], ssem.at[at], rsem.at[at], peer(j))
 
     def come(k, j):
         at = (1, k, j)
-        return remote(turned.at[k, (e + j) % GROUPS], landed.at[k, e], ssem.at[at], rsem.at[at], peer(j))
+        return remote(turned[k].at[(e + j) % GROUPS], landed[k].at[e], ssem.at[at], rsem.at[at], peer(j))
 
     def permute(arrived, to):
         def step(p, carry):
@@ -547,17 +613,16 @@
 
         lax.fori_loop(0, GROUPS, step, 0)
 
-    for h, run in enumerate(runs):
-        pack(lead_out[h].at[e], run[1], update(e, *run)[0])
+    pack_lead(e)
     pl.semaphore_wait(barrier, 2 * GROUPS + 1)
-    for h, run in enumerate(runs):
-
-        def first_leg(j, h=h, run=run):
-            g = (e + j) % GROUPS
-            pack(lead_out[h].at[g], run[1], update(g, *run)[0])
-            lead_go(h, j).start()
-
-        each(first_leg)
+
+    def first_leg(j):
+        pack_lead((e + j) % GROUPS)
+        lead_go(0, j).start()
+
+    each(first_leg)
+    each(lambda j: lead_go(1, j).start())
+    for h in range(2):
         lead_mid[h][0] = lead_out[h][e]
 
     for h in range(2):
@@ -570,8 +635,11 @@
 
     def moments(g):
         _, first_new, second_new = update(g)
-        pack(leaving.at[0, g], rows, first_new)
-        pack(leaving.at[1, g], rows, second_new)
+        code = column_code(first_new), column_code(second_new)
+        leaving0[g, 0:rows, :] = to_codes(first_new, code[0])
+        leaving1[g] = to_codes(second_new, code[1])
+        both = [jnp.broadcast_to(c, (8, LANES)) for c in code]
+        leaving0[g, rows:, :] = jnp.concatenate(both, axis=0).astype(I16)
 
     each(moments, 0)
 
@@ -586,12 +654,12 @@
         return send(part, part, a_ssem.at[n, h], a_rsem.at[n, h], device)
 
     def settle(h, g):
-        values = unpack(lead_land[h].at[g], runs[h][1])
+        values = unpack(lead_land[h].at[g], runs[h][1], lead_land0[g, split : split + 1, :])
         new_master[pl.ds(*runs[h]), columns(g)] = values
         weight[weight_rows(own, h), columns(g)] = values.astype(jnp.bfloat16)
 
     def settle_twin(h, g):
-        values = unpack(lead_twin[h].at[g], runs[h][1])
+        values = unpack(lead_twin[h].at[g], runs[h][1], lead_twin0[g, split : split + 1, :])
         weight[weight_rows(twin, h), columns(g)] = values.astype(jnp.bfloat16)
 
     to_right, to_left = [], []
@@ -630,10 +698,10 @@
 
     def turn(k):
         each(lambda j: go(k, j).wait_recv())
-        middle[k][0] = leaving[k, e]
-        permute(middle[k], turned.at[k])
+        middle[k][0] = leaving[k][e]
+        permute(middle[k], turned[k])
         each(lambda j: come(k, j).start())
-        landed[k, e] = turned[k, e]
+        landed[k][e] = turned[k][e]
 
     pass_on(4, 0, zl, to_right[0], to_left[0])
     pass_on(4, 1, zl, to_right[1], to_left[1])
@@ -643,16 +711,7 @@
     pass_on(6, 1, 1 - zl, twin_right[1], twin_left[1])
 
     for k in range(2):
-
-        def finish(g, k=k):
-            results[k][:, columns(g)] = unpack(landed.at[k, g], rows)
-
-        def finish_next(j, k=k, finish=finish):
-            come(k, j).wait_recv()
-            finish((e - j + GROUPS) % GROUPS)
-
-        finish(e)
-        each(finish_next)
+        each(lambda j, k=k: come(k, j).wait_recv())
     for copy in onward:
         copy.wait_recv()
     for k in range(2):
@@ -740,19 +799,18 @@
     )(in_hbm(hidden[0]), in_hbm(upstream[0]), token_counts, in_hbm(router_cot), in_hbm(router_input))
 
     clip_limit = 2.0 * math.sqrt(float(GROUPS * units * wide + n_router * wide))
-    tall = rows + 16
     split = (rows // 16 + 1) // 2 * 16
     state = jax.ShapeDtypeStruct((rows, wide), F32)
-    weight, new_master, new_first, new_second = pl.pallas_call(
+    codes = [jax.ShapeDtypeStruct((GROUPS, n, LANES), I16) for n in (rows + 16, rows)]
+    weights = jax.ShapeDtypeStruct((units, wide), jnp.bfloat16)
+    weight, new_master, *landed = pl.pallas_call(
         functools.partial(move_kernel, clip_limit),
-        out_shape=(jax.ShapeDtypeStruct((units, wide), jnp.bfloat16), state, state, state),
+        out_shape=(weights, state, *codes),
         in_specs=[vmem, vmem, vmem, vmem, vmem, smem],
         out_specs=(vmem, vmem, vmem, vmem),
         scratch_shapes=[
-            *[pltpu.VMEM((GROUPS, n, LANES), I16) for n in (split + 16, rows - split + 16)] * 5,
-            pltpu.VMEM((2, GROUPS, tall, LANES), I16),
-            *[pltpu.VMEM((GROUPS, tall, LANES), I16)] * 2,
-            *[pltpu.VMEM((2, GROUPS, tall, LANES), I16)] * 2,
+            *[pltpu.VMEM((GROUPS, n, LANES), I16) for n in (split + 16, rows - split)] * 5,
+            *[pltpu.VMEM((GROUPS, n, LANES), I16) for n in (rows + 16, rows)] * 3,
             dma((3, 2, GROUPS)),
             dma((3, 2, GROUPS)),
             dma((2, 2, GROUPS)),
@@ -766,18 +824,21 @@
         name="move",
     )(gradient, total, master[0], first_moment[0], second_moment[0], partner)
 
-    factor = jnp.minimum(1.0, clip_limit / (jnp.sqrt(total[0, 0]) + norm_eps))
-    router_outs = adam_update(factor * router_grad, router_first, router_second, router_master)
-
-    return (
-        weight[None],
-        new_master[None],
-        new_first[None],
-        new_second[None],
-        router_outs[0],
-        router_outs[1],
-        router_outs[2],
-    )
+    router = jax.ShapeDtypeStruct(router_master.shape, F32)
+    weight, new_master, new_first, new_second, *router_outs = pl.pallas_call(
+        functools.partial(close_kernel, clip_limit),
+        out_shape=(weights, state, state, state, router, router, router),
+        in_specs=[vmem] * 9,
+        out_specs=[hbm] * 7,
+        scratch_shapes=[
+            pltpu.VMEM((2, rows, wide), F32),
+            pltpu.VMEM((3, *router_master.shape), F32),
+            dma((7,)),
+        ],
+        compiler_params=pltpu.CompilerParams(vmem_limit_bytes=20 * 1024 * 1024),
+        name="close",
+    )(weight, new_master, *landed, total, router_grad, router_master, router_first, router_second)
+    return (weight[None], new_master[None], new_first[None], new_second[None], *router_outs)
 
 
 def solution(mesh):

time: 155 us -> 148 us (0.955)
  local copies, waits for them, and re-layouts: 6.38 us -> 0.04 us
  Pallas kernels: 144 us -> 147 us
    unnamed x18 -> x14, local copies, waits for them, and re-layouts: 5.86 us -> 0.04 us
    pallas_call x1 -> x2, Pallas kernels: 75.4 us -> 78.8 us  [the longest x1 74.4 us: on_device(): pl.pallas_call(functools.partial(move_kernel, clip_limit), out_shape=(wei...]
where the time goes in v4:
time: 148 us
  Pallas kernels  147 us (99%)
    pallas_call x1, Pallas kernels, on_device(): pl.pallas_call(functools.partial(move_kernel, clip_limit), out_shape=(wei...  74.4 us
    pallas_call x1, Pallas kernels, on_device(): pl.pallas_call(reduce_kernel, out_shape=(jax.ShapeDtypeStruct((rows, wide...  67.9 us
    pallas_call x1, Pallas kernels, on_device(): pl.pallas_call(functools.partial(close_kernel, clip_limit), out_shape=(we...  4.37 us

profile of v4, /device:TPU:1, one launch (start us, length us, event | category | flops | bytes accessed | tf_op | source)
XLA Modules:
  0.0 148.1 jit_solution(15269935999003253475)
XLA Ops:
  1.3 0.0 copy-start
  1.3 0.0 copy-start.1
  1.3 0.0 copy-start.2
  1.3 0.0 copy-start.6
  1.3 67.9 %reduce.1 = (f32[176,2048]{1,0:T(8,128)S(1)}, f32[64,2048]{1,0:T(8,128)S(1)}, f32[8,128]{1,0:T(8,128)S(1)}) custom-call(bf16[1152,1408]{1,0:T(8,128)(2,1)} %bitcast.13, bf16[1152,2048]{1,0:T(8,128)(2,1)} %bitcast.12, s32[1,1]{1,0:T(1,128)S(6)} %copy.19.counts, bf16[64,128]{1,0:T(8,128)(2,1)} %cot_hbm.1, bf16[128,2048]{1,0:T(8,128)(2,1)} %rin_hbm.1), custom_call_target="tpu_custom_call" | custom-call | tf_op jit(solution)/shard_map/reduce/pallas_call | solution.py:754
  69.2 0.0 copy-done
  69.3 0.0 copy-done.1
  69.3 0.0 copy-done.2
  69.3 0.0 copy-done.6
  69.3 0.0 copy-start.3
  69.3 0.0 copy-start.4
  69.3 0.0 copy-start.5
  69.3 74.4 %move.1 = (bf16[1408,2048]{1,0:T(8,128)(2,1)S(1)}, f32[176,2048]{1,0:T(8,128)S(1)}, s16[16,192,128]{2,1,0:T(8,128)(2,1)S(1)}, s16[16,176,128]{2,1,0:T(8,128)(2,1)S(1)}) custom-call(f32[176,2048]{1,0:T(8,128)S(1)} %get-tuple-element.21.grad, f32[8,128]{1,0:T(8,128)S(1)} %get-tuple-element.22.total, f32[176,2048]{1,0:T(8,128)S(1)} %bitcast.9, ...), custom_call_target="tpu_custom_call" | custom-call | tf_op jit(solution)/shard_map/move/pallas_call | solution.py:806
  143.7 0.0 copy-done.3
  143.7 0.0 copy-done.4
  143.7 0.0 copy-done.5
  143.8 4.4 %close.1 = (bf16[1408,2048]{1,0:T(8,128)(2,1)}, f32[176,2048]{1,0:T(8,128)}, f32[176,2048]{1,0:T(8,128)}, f32[176,2048]{1,0:T(8,128)}, f32[64,2048]{1,0:T(8,128)...) custom-call(bf16[1408,2048]{1,0:T(8,128)(2,1)S(1)} %get-tuple-element.23.weight, f32[176,2048]{1,0:T(8,128)S(1)} %get-tuple-element.24.new_master, ...), custom_call_target="tpu_custom_call" | custom-call | tf_op jit(solution)/shard_map/close/pallas_call | solution.py:828
Async XLA Ops:
  1.3 68.0 %copy-start = (f32[1,176,2048]{2,1,0:T(8,128)S(1)}, f32[1,176,2048]{2,1,0:T(8,128)}, u32[]{:S(2)}) copy-start(f32[1,176,2048]{2,1,0:T(8,128)} %param.15) | copy-start | bytes 4325380
  1.3 68.0 %copy-start.1 = (f32[1,176,2048]{2,1,0:T(8,128)S(1)}, f32[1,176,2048]{2,1,0:T(8,128)}, u32[]{:S(2)}) copy-start(f32[1,176,2048]{2,1,0:T(8,128)} %param.16) | copy-start | bytes 4325380
  1.3 68.0 %copy-start.2 = (f32[1,176,2048]{2,1,0:T(8,128)S(1)}, f32[1,176,2048]{2,1,0:T(8,128)}, u32[]{:S(2)}) copy-start(f32[1,176,2048]{2,1,0:T(8,128)} %param.17) | copy-start | bytes 4325380
  1.3 68.0 %copy-start.6 = (s32[16]{0:T(128)S(1)}, s32[16]{0:T(128)}, u32[]{:S(2)}) copy-start(s32[16]{0:T(128)} %partner.1) | copy-start | bytes 196
  69.3 74.4 %copy-start.3 = (f32[64,2048]{1,0:T(8,128)S(1)}, f32[64,2048]{1,0:T(8,128)}, u32[]{:S(2)}) copy-start(f32[64,2048]{1,0:T(8,128)} %r_master.1) | copy-start | bytes 1572868
  69.3 74.4 %copy-start.4 = (f32[64,2048]{1,0:T(8,128)S(1)}, f32[64,2048]{1,0:T(8,128)}, u32[]{:S(2)}) copy-start(f32[64,2048]{1,0:T(8,128)} %r_first.1) | copy-start | bytes 1572868
  69.3 74.4 %copy-start.5 = (f32[64,2048]{1,0:T(8,128)S(1)}, f32[64,2048]{1,0:T(8,128)}, u32[]{:S(2)}) copy-start(f32[64,2048]{1,0:T(8,128)} %r_second.1) | copy-start | bytes 1572868

commit v5 on v4

--- a/solution.py
+++ b/solution.py
@@ -28,6 +28,7 @@
 LANES = 128
 TOP = 15.0
 SMALL = 2.0**-100
+MOVE_SCRATCH = 22
 
 
 def code_of(peak):
@@ -63,13 +64,21 @@
     return copy
 
 
+def each(act, start=1):
+    def step(j, carry):
+        act(j)
+        return carry
+
+    lax.fori_loop(start, GROUPS, step, 0)
+
+
 def reduce_kernel(
+    states,
     hid_hbm,
     up_hbm,
     counts,
     cot_hbm,
     rin_hbm,
-    grad,
     rgrad,
     total,
     hid,
@@ -147,9 +156,14 @@
     for copy in loads:
         copy.start()
     barrier = pltpu.get_barrier_semaphore()
-    for at, size in ((at_plane, 16), (at_side, 8)):
-        for j in range(1, size):
-            pl.semaphore_signal(barrier, inc=1, device_id=at(j), device_id_type=MESH)
+    for j in range(1, 16):
+        pl.semaphore_signal(barrier, inc=1, device_id=at_plane(j), device_id_type=MESH)
+
+    def greet(device):
+        pl.semaphore_signal(barrier, inc=1, device_id=device, device_id_type=MESH)
+
+    each(lambda j: greet({"e": (e + j) % GROUPS}))
+    each(lambda j: greet({"e": (e + j) % GROUPS, "zl": 1 - zl}), 0)
 
     live = counts[0, 0]
     keep = (lax.broadcasted_iota(jnp.int32, (depth, LANES), 0) < live).astype(F32).astype(jnp.bfloat16)
@@ -239,7 +253,7 @@
 
     loads[1].wait()
     multiply((1 - zl) * 4 + far)
-    pl.semaphore_wait(barrier, 22)
+    pl.semaphore_wait(barrier, 15 + 15 + 16)
     p0 = pair_part(0, far)
     early_part((1 - zl) * 4 + far, 1 - zl, 1 + 2 * zl)
     multiply(zl * 4 + far)
@@ -291,6 +305,11 @@
     l0 = late_part(far, a_at, late_a, 0, 3)
     l1 = late_part(far, b_at, late_b, 1, 1)
 
+    held = [terms.at[block] for block in (far, 4 + far, (1 - zl) * 4 + right)]
+    state_loads = [pltpu.make_async_copy(src, dst, states[3].at[k]) for k, (src, dst) in enumerate(zip(states, held))]
+    for copy in state_loads:
+        copy.start()
+
     for copy in s1:
         copy.wait_recv()
     r2[...] = r1[pl.ds(pl.multiple_of(y * 8, 8), 8), :] + r_in1[0] + r_in1[1] + r_in1[2]
@@ -377,7 +396,7 @@
             values = terms[own, r, :]
             for source in sources:
                 values = values + decode_rows(source, i, wide)
-            grad[r, :] = values
+            terms[own, r, :] = values
             return count(values, acc)
 
         return lax.fori_loop(0, size // 16, step, acc, unroll=True)
@@ -423,6 +442,20 @@
     waits = [e0, e1, e2, e3, e4, e5, l0, l1, l2, l3, l4, l5, p0, p1, p2, p3, last, s0, *s1, *s2, *s3]
     for copy in waits + b0 + b1 + b2 + b3 + plane_copies + side_copies:
         copy.wait_send()
+    return state_loads, terms.at[own], held
+
+
+def step_kernel(limit, *refs):
+    (hid, up, counts, cot, rin, master_hbm, first_hbm, second_hbm, partner), refs = refs[:9], refs[9:]
+    (rgrad, total, weight, new_master, landed0, landed1), refs = refs[:6], refs[6:]
+    state_sem, refs = refs[0], refs[1:]
+    n = len(refs) - MOVE_SCRATCH
+    states = (master_hbm, first_hbm, second_hbm, state_sem)
+    loads, grad, held = reduce_kernel(states, hid, up, counts, cot, rin, rgrad, total, *refs[:n])
+    for copy in loads:
+        copy.wait()
+    outs = (weight, new_master, landed0, landed1)
+    move_kernel(limit, grad, total, *held, partner, *outs, *refs[n:])
 
 
 def adam_update(gradient, moment_one, moment_two, weights):
@@ -435,14 +468,6 @@
 
 def in_hbm(array):
     return pltpu.with_memory_space_constraint(array, pltpu.HBM)
-
-
-def each(act, start=1):
-    def step(j, carry):
-        act(j)
-        return carry
-
-    lax.fori_loop(start, GROUPS, step, 0)
 
 
 def unpack(piece, size, codes):
@@ -549,12 +574,6 @@
     def at_x(j):
         return {"x": (x + j) % 4}
 
-    barrier = pltpu.get_barrier_semaphore()
-    each(lambda j: pl.semaphore_signal(barrier, inc=1, device_id=peer(j), device_id_type=MESH))
-    each(lambda j: pl.semaphore_signal(barrier, inc=1, device_id=twin_peer(j), device_id_type=MESH), 0)
-    for device in (at_x(1), at_x(3)):
-        pl.semaphore_signal(barrier, inc=1, device_id=device, device_id_type=MESH)
-
     factor = jnp.minimum(1.0, limit / (jnp.sqrt(total[0:1, 0:1]) + norm_eps))
 
     def columns(g):
@@ -614,7 +633,6 @@
         lax.fori_loop(0, GROUPS, step, 0)
 
     pack_lead(e)
-    pl.semaphore_wait(barrier, 2 * GROUPS + 1)
 
     def first_leg(j):
         pack_lead((e + j) % GROUPS)
@@ -751,16 +769,24 @@
     late = rows * 5 // 11 // 16 * 16
     early = rows - late
     late_a = (late // 16 + 1) // 2 * 16
-    gradient, router_grad, total = pl.pallas_call(
-        reduce_kernel,
+    clip_limit = 2.0 * math.sqrt(float(GROUPS * units * wide + n_router * wide))
+    split = (rows // 16 + 1) // 2 * 16
+    state = jax.ShapeDtypeStruct((rows, wide), F32)
+    codes = [jax.ShapeDtypeStruct((GROUPS, n, LANES), I16) for n in (rows + 16, rows)]
+    weights = jax.ShapeDtypeStruct((units, wide), jnp.bfloat16)
+    router_grad, total, weight, new_master, *landed = pl.pallas_call(
+        functools.partial(step_kernel, clip_limit),
         out_shape=(
-            jax.ShapeDtypeStruct((rows, wide), F32),
             jax.ShapeDtypeStruct((n_router, wide), F32),
             jax.ShapeDtypeStruct((8, LANES), F32),
+            weights,
+            state,
+            *codes,
         ),
-        in_specs=[hbm, hbm, smem, hbm, hbm],
-        out_specs=(vmem, vmem, vmem),
+        in_specs=[hbm, hbm, smem, hbm, hbm, hbm, hbm, hbm, smem],
+        out_specs=(vmem,) * 6,
         scratch_shapes=[
+            dma((3,)),
             pltpu.VMEM((depth, units), jnp.bfloat16),
             pltpu.VMEM((depth, wide), jnp.bfloat16),
             pltpu.VMEM(router_cot.shape, jnp.bfloat16),
@@ -791,24 +817,6 @@
             dma((8, 4)),
             dma((24,)),
             dma((24,)),
-        ],
-        compiler_params=pltpu.CompilerParams(
-            collective_id=0, has_side_effects=True, vmem_limit_bytes=40 * 1024 * 1024
-        ),
-        name="reduce",
-    )(in_hbm(hidden[0]), in_hbm(upstream[0]), token_counts, in_hbm(router_cot), in_hbm(router_input))
-
-    clip_limit = 2.0 * math.sqrt(float(GROUPS * units * wide + n_router * wide))
-    split = (rows // 16 + 1) // 2 * 16
-    state = jax.ShapeDtypeStruct((rows, wide), F32)
-    codes = [jax.ShapeDtypeStruct((GROUPS, n, LANES), I16) for n in (rows + 16, rows)]
-    weights = jax.ShapeDtypeStruct((units, wide), jnp.bfloat16)
-    weight, new_master, *landed = pl.pallas_call(
-        functools.partial(move_kernel, clip_limit),
-        out_shape=(weights, state, *codes),
-        in_specs=[vmem, vmem, vmem, vmem, vmem, smem],
-        out_specs=(vmem, vmem, vmem, vmem),
-        scratch_shapes=[
             *[pltpu.VMEM((GROUPS, n, LANES), I16) for n in (split + 16, rows - split)] * 5,
             *[pltpu.VMEM((GROUPS, n, LANES), I16) for n in (rows + 16, rows)] * 3,
             dma((3, 2, GROUPS)),
@@ -819,10 +827,20 @@
             dma((8, 2)),
         ],
         compiler_params=pltpu.CompilerParams(
-            collective_id=1, has_side_effects=True, vmem_limit_bytes=27 * 1024 * 1024
+            collective_id=0, has_side_effects=True, vmem_limit_bytes=44 * 1024 * 1024
         ),
-        name="move",
-    )(gradient, total, master[0], first_moment[0], second_moment[0], partner)
+        name="step",
+    )(
+        in_hbm(hidden[0]),
+        in_hbm(upstream[0]),
+        token_counts,
+        in_hbm(router_cot),
+        in_hbm(router_input),
+        in_hbm(master[0]),
+        in_hbm(first_moment[0]),
+        in_hbm(second_moment[0]),
+        partner,
+    )
 
     router = jax.ShapeDtypeStruct(router_master.shape, F32)
     weight, new_master, new_first, new_second, *router_outs = pl.pallas_call(

time: 148 us -> 146 us (0.986)
  Pallas kernels: 147 us -> 144 us
    pallas_call x2 -> x1, Pallas kernels: 142 us -> 139 us  [on_device(): pl.pallas_call(functools.partial(step_kernel, clip_limit), out_shape=(jax...]
where the time goes in v5:
time: 146 us
  Pallas kernels  144 us (99%)
    pallas_call x1, Pallas kernels, on_device(): pl.pallas_call(functools.partial(step_kernel, clip_limit), out_shape=(jax...  139 us
    pallas_call x1, Pallas kernels, on_device(): pl.pallas_call(functools.partial(close_kernel, clip_limit), out_shape=(we...  4.37 us

profile of v5, /device:TPU:1, one launch (start us, length us, event | category | flops | bytes accessed | tf_op | source)
XLA Modules:
  0.0 145.5 jit_solution(12387218375985047659)
XLA Ops:
  1.3 0.0 copy-start.3
  1.3 0.6 copy-done.3
  1.9 0.0 copy-start
  1.9 0.0 copy-start.1
  1.9 0.0 copy-start.2
  1.9 139.2 %step.1 = (f32[64,2048]{1,0:T(8,128)S(1)}, f32[8,128]{1,0:T(8,128)S(1)}, bf16[1408,2048]{1,0:T(8,128)(2,1)S(1)}, f32[176,2048]{1,0:T(8,128)S(1)}, s16[16,192,128...) custom-call(bf16[1152,1408]{1,0:T(8,128)(2,1)} %bitcast.10, bf16[1152,2048]{1,0:T(8,128)(2,1)} %bitcast.9, ...), custom_call_target="tpu_custom_call" | custom-call | tf_op jit(solution)/shard_map/step/pallas_call | solution.py:777
  141.1 0.0 copy-done
  141.1 0.0 copy-done.1
  141.1 0.0 copy-done.2
  141.1 4.4 %close.1 = (bf16[1408,2048]{1,0:T(8,128)(2,1)}, f32[176,2048]{1,0:T(8,128)}, f32[176,2048]{1,0:T(8,128)}, f32[176,2048]{1,0:T(8,128)}, f32[64,2048]{1,0:T(8,128)...) custom-call(bf16[1408,2048]{1,0:T(8,128)(2,1)S(1)} %get-tuple-element.20.weight, f32[176,2048]{1,0:T(8,128)S(1)} %get-tuple-element.21.new_master, ...), custom_call_target="tpu_custom_call" | custom-call | tf_op jit(solution)/shard_map/close/pallas_call | solution.py:846
Async XLA Ops:
  1.3 0.7 copy-start.3
  1.9 139.2 %copy-start = (f32[64,2048]{1,0:T(8,128)S(1)}, f32[64,2048]{1,0:T(8,128)}, u32[]{:S(2)}) copy-start(f32[64,2048]{1,0:T(8,128)} %r_master.1) | copy-start | bytes 1572868
  1.9 139.2 %copy-start.1 = (f32[64,2048]{1,0:T(8,128)S(1)}, f32[64,2048]{1,0:T(8,128)}, u32[]{:S(2)}) copy-start(f32[64,2048]{1,0:T(8,128)} %r_first.1) | copy-start | bytes 1572868
  1.9 139.2 %copy-start.2 = (f32[64,2048]{1,0:T(8,128)S(1)}, f32[64,2048]{1,0:T(8,128)}, u32[]{:S(2)}) copy-start(f32[64,2048]{1,0:T(8,128)} %r_second.1) | copy-start | bytes 1572868

commit v6 on v5

--- a/solution.py
+++ b/solution.py
@@ -66,7 +66,7 @@
 
 def each(act, start=1):
     def step(j, carry):
-        act(j)
+        act(j * (GROUPS - 1) % GROUPS)
         return carry
 
     lax.fori_loop(start, GROUPS, step, 0)

time: 146 us -> 145 us (level)
  Pallas kernels: 144 us -> 142 us
where the time goes in v6:
time: 145 us; the launch traced here: 144 us
  Pallas kernels  142 us (98%)
    pallas_call x1, Pallas kernels, on_device(): pl.pallas_call(functools.partial(step_kernel, clip_limit), out_shape=(jax...  138 us
    pallas_call x1, Pallas kernels, on_device(): pl.pallas_call(functools.partial(close_kernel, clip_limit), out_shape=(we...  4.37 us

profile of v6, /device:TPU:1, one launch (start us, length us, event | category | flops | bytes accessed | tf_op | source)
XLA Modules:
  0.0 144.4 jit_solution(4161662247513750289)
XLA Ops:
  1.3 0.0 copy-start.3
  1.3 0.6 copy-done.3
  1.9 0.0 copy-start
  1.9 0.0 copy-start.1
  1.9 0.0 copy-start.2
  1.9 138.1 %step.1 = (f32[64,2048]{1,0:T(8,128)S(1)}, f32[8,128]{1,0:T(8,128)S(1)}, bf16[1408,2048]{1,0:T(8,128)(2,1)S(1)}, f32[176,2048]{1,0:T(8,128)S(1)}, s16[16,192,128...) custom-call(bf16[1152,1408]{1,0:T(8,128)(2,1)} %bitcast.10, bf16[1152,2048]{1,0:T(8,128)(2,1)} %bitcast.9, ...), custom_call_target="tpu_custom_call" | custom-call | tf_op jit(solution)/shard_map/step/pallas_call | solution.py:777
  140.0 0.0 copy-done
  140.1 0.0 copy-done.1
  140.1 0.0 copy-done.2
  140.1 4.4 %close.1 = (bf16[1408,2048]{1,0:T(8,128)(2,1)}, f32[176,2048]{1,0:T(8,128)}, f32[176,2048]{1,0:T(8,128)}, f32[176,2048]{1,0:T(8,128)}, f32[64,2048]{1,0:T(8,128)...) custom-call(bf16[1408,2048]{1,0:T(8,128)(2,1)S(1)} %get-tuple-element.20.weight, f32[176,2048]{1,0:T(8,128)S(1)} %get-tuple-element.21.new_master, ...), custom_call_target="tpu_custom_call" | custom-call | tf_op jit(solution)/shard_map/close/pallas_call | solution.py:846
Async XLA Ops:
  1.3 0.7 copy-start.3
  1.9 138.1 %copy-start = (f32[64,2048]{1,0:T(8,128)S(1)}, f32[64,2048]{1,0:T(8,128)}, u32[]{:S(2)}) copy-start(f32[64,2048]{1,0:T(8,128)} %r_master.1) | copy-start | bytes 1572868
  1.9 138.1 %copy-start.1 = (f32[64,2048]{1,0:T(8,128)S(1)}, f32[64,2048]{1,0:T(8,128)}, u32[]{:S(2)}) copy-start(f32[64,2048]{1,0:T(8,128)} %r_first.1) | copy-start | bytes 1572868
  1.9 138.1 %copy-start.2 = (f32[64,2048]{1,0:T(8,128)S(1)}, f32[64,2048]{1,0:T(8,128)}, u32[]{:S(2)}) copy-start(f32[64,2048]{1,0:T(8,128)} %r_second.1) | copy-start | bytes 1572868
